TPU v7x, 32 devices: a whole 2x2x4 slice. The times are simulated.
32 devices in a mesh: dp: 8 (over y, x, core), seq: 4 (over z).
Axes of the slice: x: 2, y: 2, z: 4, core: 2. Of those that a mesh axis runs over, the one named last changes fastest.
Arguments:
- query_rows: bfloat16 [8, 512, 3072], P('dp', 'seq'), may hold values from -6 to 6
- key_rows: bfloat16 [8, 512, 3072], P('dp', 'seq'), may hold values from -6 to 6
- value_rows: bfloat16 [8, 512, 3072], P('dp', 'seq'), may hold values from -6 to 6
- out_grad: bfloat16 [8, 512, 6144], P('dp', 'seq'), may hold values from -54 to 54
- clip_lengths: int32 [8, 4], P('dp'), may hold values from 1 to 256, 512 in all within a row
- out_weight: bfloat16 [3072, 6144], P('seq'), may hold values from -0.109375 to 0.109375
- query_gain: float32 [128], replicated, may hold values from 0.1 to 1.9
- key_gain: float32 [128], replicated, may hold values from 0.1 to 1.9
Outputs:
- query_grad: bfloat16 [8, 512, 3072], P('dp', 'seq')
- key_grad: bfloat16 [8, 512, 3072], P('dp', 'seq')
- value_grad: bfloat16 [8, 512, 3072], P('dp', 'seq')
- weight_grad: float32 [3072, 6144], P('seq', 'dp')
- querygain_grad: float32 [128], replicated
- keygain_grad: float32 [128], replicated
- grad_norm: float32 [], replicated
Inputs may be any that keep to these rules, and one draw needn't show every extreme that they name: `clip_lengths`: the token counts of each group's clips sum to 512.
All inputs are finite; a program needn't handle non-finite values.
Results may differ from a plain program's by a relative error of at most 0.015.
Values may be sent and summed in bfloat16 or wider, within the bound.
No kernel may reach another device: no remote copies, remote signals or barrier semaphores. Data moves between devices by JAX's collectives and lax.ppermute only.
A program may use at most 128 MiB of HBM per device.

v0:
```python
import jax
import jax.numpy as jnp
from jax import lax
from jax.sharding import PartitionSpec as P

HEAD_DIM = 128
MAX_NORM = 768


EPS = 1e-06


def segment_ids(lengths, total):
    ends = jnp.cumsum(lengths)
    places = jnp.arange(total, dtype=jnp.int32)
    return jnp.sum((places[:, None] >= ends[None, :]).astype(jnp.int32), axis=1)


def norm_rows(rows, gain):
    wide = rows.astype(jnp.float32)
    inverse = lax.rsqrt(jnp.mean(wide * wide, axis=-1, keepdims=True) + EPS)
    unit = wide * inverse
    return (unit, inverse, (unit * gain).astype(jnp.bfloat16))


def norm_back(unit, inverse, gain, d_norm):
    gain_part = jnp.sum(unit * d_norm, axis=(0, 1))
    d_unit = d_norm * gain
    d_rows = inverse * (d_unit - unit * jnp.mean(unit * d_unit, axis=-1, keepdims=True))
    return (d_rows.astype(jnp.bfloat16), gain_part)


def local(
    query_rows, key_rows, value_rows, out_grad, clip_lengths, out_weight, query_gain, key_gain
):
    query, keys, values = (
        lax.all_to_all(query_rows[0], "seq", split_axis=1, concat_axis=0, tiled=True),
        lax.all_to_all(key_rows[0], "seq", split_axis=1, concat_axis=0, tiled=True),
        lax.all_to_all(value_rows[0], "seq", split_axis=1, concat_axis=0, tiled=True),
    )
    total = query.shape[0]
    heads = query.shape[1] // HEAD_DIM
    width = heads * HEAD_DIM
    scale = HEAD_DIM ** (-0.5)
    block = min(512, total)
    blocks = total // block
    seg = segment_ids(clip_lengths[0], total)
    q_unit, q_inv, q_norm = norm_rows(query.reshape(total, heads, HEAD_DIM), query_gain)
    k_unit, k_inv, k_norm = norm_rows(keys.reshape(total, heads, HEAD_DIM), key_gain)
    values3 = values.reshape(total, heads, HEAD_DIM)

    def forward_block(index):
        start = index * block
        query_block = lax.dynamic_slice_in_dim(q_norm, start, block, 0)
        seg_block = lax.dynamic_slice_in_dim(seg, start, block, 0)
        scores = (
            jnp.einsum("qhd,khd->hqk", query_block, k_norm, preferred_element_type=jnp.float32)
            * scale
        )
        same = seg_block[:, None] == seg[None, :]
        expo = jnp.where(same[None], jnp.exp(scores), 0.0)
        probs = (expo / jnp.sum(expo, axis=-1, keepdims=True)).astype(jnp.bfloat16)
        attn_out = jnp.einsum("hqk,khd->qhd", probs, values3, preferred_element_type=jnp.float32)
        return (probs, attn_out.astype(jnp.bfloat16))

    probs_all, attn_blocks = lax.map(forward_block, jnp.arange(blocks, dtype=jnp.int32))
    attn_flat = attn_blocks.reshape(total, width)
    out_full = lax.all_gather(out_grad[0], "seq", axis=0, tiled=True)
    weight_part = jnp.dot(attn_flat.T, out_full, preferred_element_type=jnp.float32)
    d_attn = jnp.dot(out_full, out_weight.T, preferred_element_type=jnp.float32).astype(
        jnp.bfloat16
    )
    d_attn3 = d_attn.reshape(total, heads, HEAD_DIM)

    def backward_block(carry, items):
        d_key, d_value = carry
        probs, index = items
        start = index * block
        attn_grad = lax.dynamic_slice_in_dim(d_attn3, start, block, 0)
        query_block = lax.dynamic_slice_in_dim(q_norm, start, block, 0)
        d_probs = jnp.einsum("qhd,khd->hqk", attn_grad, values3, preferred_element_type=jnp.float32)
        probs32 = probs.astype(jnp.float32)
        row_sum = jnp.sum(probs32 * d_probs, axis=-1, keepdims=True)
        d_scores = (probs32 * (d_probs - row_sum) * scale).astype(jnp.bfloat16)
        d_value = d_value + jnp.einsum(
            "hqk,qhd->khd", probs, attn_grad, preferred_element_type=jnp.float32
        )
        d_key = d_key + jnp.einsum(
            "hqk,qhd->khd", d_scores, query_block, preferred_element_type=jnp.float32
        )
        d_query = jnp.einsum("hqk,khd->qhd", d_scores, k_norm, preferred_element_type=jnp.float32)
        return ((d_key, d_value), d_query)

    empty = jnp.zeros((total, heads, HEAD_DIM), jnp.float32)
    (d_knorm, d_value32), d_query_blocks = lax.scan(
        backward_block, (empty, empty), (probs_all, jnp.arange(blocks, dtype=jnp.int32))
    )
    d_qnorm = d_query_blocks.reshape(total, heads, HEAD_DIM)
    query_grad, q_gain_part = norm_back(q_unit, q_inv, query_gain, d_qnorm)
    key_grad, k_gain_part = norm_back(k_unit, k_inv, key_gain, d_knorm)
    value_grad = d_value32.astype(jnp.bfloat16)
    query_back, key_back, value_back = (
        lax.all_to_all(
            query_grad.reshape(total, width), "seq", split_axis=0, concat_axis=1, tiled=True
        ),
        lax.all_to_all(
            key_grad.reshape(total, width), "seq", split_axis=0, concat_axis=1, tiled=True
        ),
        lax.all_to_all(
            value_grad.reshape(total, width), "seq", split_axis=0, concat_axis=1, tiled=True
        ),
    )
    weight_shard = lax.psum_scatter(
        weight_part.astype(jnp.bfloat16), "dp", scatter_dimension=1, tiled=True
    ).astype(jnp.float32)
    local_squares = jnp.sum(weight_shard * weight_shard)
    qgain_raw, kgain_raw = lax.psum((q_gain_part, k_gain_part), ("dp", "seq"))
    weight_squares = lax.psum(local_squares, ("dp", "seq"))
    squares = weight_squares + jnp.sum(qgain_raw * qgain_raw) + jnp.sum(kgain_raw * kgain_raw)
    grad_norm = jnp.sqrt(squares)
    factor = jnp.minimum(jnp.float32(1.0), MAX_NORM / (grad_norm + EPS))
    return (
        query_back[None],
        key_back[None],
        value_back[None],
        weight_shard * factor,
        qgain_raw * factor,
        kgain_raw * factor,
        grad_norm,
    )


def solution(mesh):
    placed = (
        P("dp", "seq", None),
        P("dp", "seq", None),
        P("dp", "seq", None),
        P("dp", "seq", None),
        P("dp", None),
        P("seq", None),
        P(),
        P(),
    )
    return jax.shard_map(
        local,
        mesh=mesh,
        in_specs=placed,
        out_specs=(
            P("dp", "seq", None),
            P("dp", "seq", None),
            P("dp", "seq", None),
            P("seq", "dp"),
            P(),
            P(),
            P(),
        ),
        check_vma=False,
    )
```

profile of v0, /device:TPU:12, one launch (start us, length us, event | category | flops | bytes accessed | tf_op | source)
XLA Modules:
  0.0 344.6 jit_solution(10818946303630261797)
XLA Ops:
  9.5 5.3 %all-to-all-start = ((bf16[128,4,768]{0,2,1:T(8,128)(2,1)}), bf16[128,4,768]{0,2,1:T(8,128)(2,1)S(1)}, u32[]{:S(2)}, u32[]{:S(2)}) async-start(bf16[128,4,768]{0,2,1:T(8,128)(2,1)} %bitcast), calls=%async_computation | async-start | bytes 1572864 | tf_op jit(solution)/shard_map/all_to_all | solution.py:37
  15.9 34.2 %all-to-all-done = bf16[128,4,768]{0,2,1:T(8,128)(2,1)S(1)} async-done(((bf16[128,4,768]{0,2,1:T(8,128)(2,1)}), bf16[128,4,768]{0,2,1:T(8,128)(2,1)S(1)}, u32[]{:S(2)}, u32[]{:S(2)}) %all-to-all-start) | async-done | bytes 786464 | tf_op jit(solution)/shard_map/all_to_all | solution.py:37
  50.1 8.0 %all-to-all-start.1 = ((bf16[128,4,768]{0,2,1:T(8,128)(2,1)}), bf16[128,4,768]{0,2,1:T(8,128)(2,1)S(1)}, u32[]{:S(2)}, u32[]{:S(2)}) async-start(bf16[128,4,768]{0,2,1:T(8,128)(2,1)} %bitcast.2), calls=%async_computation.1 | async-start | bytes 1572864 | tf_op jit(solution)/shard_map/all_to_all | solution.py:38
  59.3 36.6 %all-to-all-done.1 = bf16[128,4,768]{0,2,1:T(8,128)(2,1)S(1)} async-done(((bf16[128,4,768]{0,2,1:T(8,128)(2,1)}), bf16[128,4,768]{0,2,1:T(8,128)(2,1)S(1)}, u32[]{:S(2)}, u32[]{:S(2)}) %all-to-all-start.1) | async-done | bytes 786464 | tf_op jit(solution)/shard_map/all_to_all | solution.py:38
  96.0 6.1 %all-to-all-start.2 = ((bf16[128,4,768]{0,2,1:T(8,128)(2,1)}), bf16[128,4,768]{0,2,1:T(8,128)(2,1)}, u32[]{:S(2)}, u32[]{:S(2)}) async-start(bf16[128,4,768]{0,2,1:T(8,128)(2,1)} %bitcast.8), calls=%async_computation.2 | async-start | bytes 1572864 | tf_op jit(solution)/shard_map/all_to_all | solution.py:39
  110.2 31.4 %all-to-all-done.2 = bf16[128,4,768]{0,2,1:T(8,128)(2,1)} async-done(((bf16[128,4,768]{0,2,1:T(8,128)(2,1)}), bf16[128,4,768]{0,2,1:T(8,128)(2,1)}, u32[]{:S(2)}, u32[]{:S(2)}) %all-to-all-start.2) | async-done | bytes 786464 | tf_op jit(solution)/shard_map/all_to_all | solution.py:39
  141.6 2.6 copy.73
  151.9 14.7 %all-gather.3.cloned.1.call-done = bf16[1,512,6144]{2,1,0:T(8,128)(2,1)} async-done(((bf16[1,128,6144]{2,1,0:T(8,128)(2,1)}), bf16[1,512,6144]{2,1,0:T(8,128)(2,1)}) %all-gather.3.cloned.1.call-update) | async-done | bytes 6291472 | tf_op jit(solution)/shard_map/all_gather | solution.py:68
  166.6 9.6 %convolution_convert_fusion = bf16[768,6144]{1,0:T(8,128)(2,1)} fusion(bf16[512,768]{0,1:T(8,128)(2,1)} %bitcast.73, bf16[1,512,6144]{2,1,0:T(8,128)(2,1)} %all-gather.3.cloned.1.call-done), kind=kOutput, calls=%fused_computation.1 | convolution fusion | flops 4836556800 | bytes 16515072 | tf_op jit(solution)/shard_map/dot_general | solution.py:69
  176.2 10.7 %fusion.13 = bf16[512,768]{1,0:T(8,128)(2,1)} fusion(bf16[768,6144]{1,0:T(8,128)(2,1)} %param.13, bf16[1,512,6144]{2,1,0:T(8,128)(2,1)} %all-gather.3.cloned.1.call-done), kind=kOutput, calls=%fused_computation.36 | convolution fusion | flops 4832231424 | bytes 16515072 | tf_op jit(solution)/shard_map/dot_general | solution.py:70
  189.3 5.9 %fusion.22 = f32[6,512,512]{1,2,0:T(8,128)} fusion(bf16[512,6,128]{0,2,1:T(8,128)(2,1)} %bitcast.70, bf16[512,6,128]{0,2,1:T(8,128)(2,1)} %reshape.149), kind=kOutput, calls=%fused_computation.54 | convolution fusion | flops 402653184 | bytes 7864320 | tf_op jit(solution)/shard_map/while/body/eval_jaxpr/qhd,khd->hqk/dot_general | solution.py:81
  195.2 9.3 %fusion.12 = (f32[128]{0:T(128)S(1)}, f32[512,6]{0,1:T(8,128)S(1)}, f32[6,128,512]{2,1,0:T(8,128)}) fusion(f32[512,6,128]{0,2,1:T(8,128)} %copy-done, f32[512,6]{0,1:T(8,128)S(1)} %get-tuple-element.81, f32[128]{0:T(128)S(1)} %copy-done.8, bf16[6,512,512]{1,2,0:T(8,128)(2,1)S(1)} %divide_convert_fusion, f32[6,512,512]{1,2,0:T(8,128)} %fusion.22, ...), kind=kOutput, calls=%fused_computation.23 | convolution fusion | flops 417202560 | bytes 14194176 | tf_op jit(solution)/shard_map/while/body/eval_jaxpr/hqk,khd->qhd/dot_general | solution.py:91
  204.6 3.7 %multiply_convert_fusion.1 = bf16[512,6,128]{0,2,1:T(8,128)(2,1)} fusion(f32[6,128,512]{2,1,0:T(8,128)} %get-tuple-element.78, f32[512,6,128]{0,2,1:T(8,128)} %copy-done, f32[512,6]{0,1:T(8,128)S(1)} %broadcast_multiply_fusion.1, f32[128]{0:T(128)S(1)} %copy-done.8, f32[512,6]{0,1:T(8,128)S(1)} %get-tuple-element.81), kind=kLoop, calls=%fused_computation.28 | loop fusion | flops 2359296 | bytes 3957248 | tf_op jit(solution)/shard_map/convert_element_type | solution.py:30
  212.8 6.5 %all-to-all-start.3 = ((bf16[4,128,768]{1,2,0:T(8,128)(2,1)}), bf16[4,128,768]{1,2,0:T(8,128)(2,1)}, u32[]{:S(2)}, u32[]{:S(2)}) async-start(bf16[4,128,768]{1,2,0:T(8,128)(2,1)} %copy.77), calls=%async_computation.3 | async-start | bytes 1572864 | tf_op jit(solution)/shard_map/all_to_all | solution.py:103
  219.4 9.8 %fusion.11 = (f32[128]{0:T(128)S(1)}, f32[512,6]{0,1:T(8,128)S(1)}, f32[6,128,512]{2,1,0:T(8,128)}) fusion(f32[512,6,128]{0,2,1:T(8,128)} %copy-done.1, f32[512,6]{0,1:T(8,128)S(1)} %get-tuple-element.80, f32[128]{0:T(128)S(1)} %copy-done.9, bf16[6,512,512]{1,2,0:T(8,128)(2,1)S(1)} %divide_convert_fusion, f32[6,512,512]{1,2,0:T(8,128)} %fusion.22, ...), kind=kOutput, calls=%fused_computation.20 | convolution fusion | flops 417202560 | bytes 14194176 | tf_op jit(solution)/shard_map/while/body/eval_jaxpr/hqk,qhd->khd/dot_general | solution.py:88
  229.2 3.3 multiply_convert_fusion
  232.5 2.5 all_to_all.78
  237.0 7.2 %all-to-all-start.4 = ((bf16[4,128,768]{1,2,0:T(8,128)(2,1)}), bf16[4,128,768]{1,2,0:T(8,128)(2,1)}, u32[]{:S(2)}, u32[]{:S(2)}) async-start(bf16[4,128,768]{1,2,0:T(8,128)(2,1)} %copy.79), calls=%async_computation.4 | async-start | bytes 1572864 | tf_op jit(solution)/shard_map/all_to_all | solution.py:106
  244.3 3.2 fusion.16
  250.2 10.6 %all-to-all-done.4 = bf16[4,128,768]{1,2,0:T(8,128)(2,1)} async-done(((bf16[4,128,768]{1,2,0:T(8,128)(2,1)}), bf16[4,128,768]{1,2,0:T(8,128)(2,1)}, u32[]{:S(2)}, u32[]{:S(2)}) %all-to-all-start.4) | async-done | bytes 786464 | tf_op jit(solution)/shard_map/all_to_all | solution.py:106
  260.7 6.8 %all-to-all-start.5 = ((bf16[4,128,768]{1,2,0:T(8,128)(2,1)}), bf16[4,128,768]{1,2,0:T(8,128)(2,1)S(1)}, u32[]{:S(2)}, u32[]{:S(2)}) async-start(bf16[4,128,768]{1,2,0:T(8,128)(2,1)} %copy.81), calls=%async_computation.5 | async-start | bytes 1572864 | tf_op jit(solution)/shard_map/all_to_all | solution.py:109
  272.2 11.8 %all-to-all-done.5 = bf16[4,128,768]{1,2,0:T(8,128)(2,1)S(1)} async-done(((bf16[4,128,768]{1,2,0:T(8,128)(2,1)}), bf16[4,128,768]{1,2,0:T(8,128)(2,1)S(1)}, u32[]{:S(2)}, u32[]{:S(2)}) %all-to-all-start.5) | async-done | bytes 786464 | tf_op jit(solution)/shard_map/all_to_all | solution.py:109
  285.2 2.6 fusion.10
  287.7 43.1 %all-reduce = (f32[]{:T(128)}, f32[128]{0:T(128)S(1)}, f32[128]{0:T(128)S(1)}) all-reduce(f32[]{:T(128)} %fusion.10, f32[128]{0:T(128)S(1)} %get-tuple-element.71, f32[128]{0:T(128)S(1)} %get-tuple-element.69), channel_id=1, replica_groups=mesh['dp'=8,'seq'=4] {'dp','seq'}, use_global_device_ids=true, to_apply=%region_10.11 | all-reduce | flops 257 | bytes 2056 | tf_op jit(solution)/shard_map/psum | solution.py:118
  (63 shorter events, 41.7 us)
Async XLA Ops:
  7.2 1.1 copy-start.5
  7.2 159.5 %all-gather.3.cloned.1.call-start = ((), (), s32[]{:S(2)}) async-start(), calls=%async_computation.8 | async-start | bytes 7864320 | tf_op jit(solution)/shard_map/all_gather | solution.py:68
  8.3 6.5 %copy-start.6 = (bf16[1,128,3072]{2,1,0:T(8,128)(2,1)S(1)}, bf16[1,128,3072]{2,1,0:T(8,128)(2,1)}, u32[]{:S(2)}) copy-start(bf16[1,128,3072]{2,1,0:T(8,128)(2,1)} %param.9) | copy-start | bytes 2359300
  9.5 40.7 %all-to-all-start = ((bf16[128,4,768]{0,2,1:T(8,128)(2,1)}), bf16[128,4,768]{0,2,1:T(8,128)(2,1)S(1)}, u32[]{:S(2)}, u32[]{:S(2)}) async-start(bf16[128,4,768]{0,2,1:T(8,128)(2,1)} %bitcast), calls=%async_computation | async-start | bytes 1572864 | tf_op jit(solution)/shard_map/all_to_all | solution.py:37
  14.8 43.4 %copy-start.7 = (bf16[1,128,3072]{2,1,0:T(8,128)(2,1)S(1)}, bf16[1,128,3072]{2,1,0:T(8,128)(2,1)}, u32[]{:S(2)}) copy-start(bf16[1,128,3072]{2,1,0:T(8,128)(2,1)} %param.10) | copy-start | bytes 2359300
  50.1 45.8 %all-to-all-start.1 = ((bf16[128,4,768]{0,2,1:T(8,128)(2,1)}), bf16[128,4,768]{0,2,1:T(8,128)(2,1)S(1)}, u32[]{:S(2)}, u32[]{:S(2)}) async-start(bf16[128,4,768]{0,2,1:T(8,128)(2,1)} %bitcast.2), calls=%async_computation.1 | async-start | bytes 1572864 | tf_op jit(solution)/shard_map/all_to_all | solution.py:38
  58.2 43.9 %copy-start.10 = (s32[1,4]{1,0:T(1,128)S(1)}, s32[1,4]{1,0:T(1,128)}, u32[]{:S(2)}) copy-start(s32[1,4]{1,0:T(1,128)} %param.12) | copy-start | bytes 52
  96.0 6.7 %copy-start.4 = (bf16[128,4,768]{0,2,1:T(8,128)(2,1)}, bf16[128,4,768]{0,2,1:T(8,128)(2,1)S(1)}, u32[]{:S(2)}) copy-start(bf16[128,4,768]{0,2,1:T(8,128)(2,1)S(1)} %all-to-all-done.1) | copy-start | bytes 2359300
  96.0 45.6 %all-to-all-start.2 = ((bf16[128,4,768]{0,2,1:T(8,128)(2,1)}), bf16[128,4,768]{0,2,1:T(8,128)(2,1)}, u32[]{:S(2)}, u32[]{:S(2)}) async-start(bf16[128,4,768]{0,2,1:T(8,128)(2,1)} %bitcast.8), calls=%async_computation.2 | async-start | bytes 1572864 | tf_op jit(solution)/shard_map/all_to_all | solution.py:39
  102.0 183.1 %reduce-scatter.2.cloned.1.call-start = ((), (), s32[]{:S(2)}) async-start(), calls=%async_computation.7 | async-start | bytes 10616832 | tf_op jit(solution)/shard_map/reduce_scatter | solution.py:113
  104.3 42.7 %copy-start = (f32[512,6,128]{0,2,1:T(8,128)}, f32[512,6,128]{0,2,1:T(8,128)S(1)}, u32[]{:S(2)}) copy-start(f32[512,6,128]{0,2,1:T(8,128)S(1)} %reshape.151) | copy-start | bytes 4718596
  110.2 36.8 %copy-start.1 = (f32[512,6,128]{0,2,1:T(8,128)}, f32[512,6,128]{0,2,1:T(8,128)S(1)}, u32[]{:S(2)}) copy-start(f32[512,6,128]{0,2,1:T(8,128)S(1)} %reshape.152) | copy-start | bytes 4718596
  146.6 0.7 copy-start.8
  146.6 0.7 copy-start.9
  149.1 1.3 copy-start.2
  212.8 24.2 %all-to-all-start.3 = ((bf16[4,128,768]{1,2,0:T(8,128)(2,1)}), bf16[4,128,768]{1,2,0:T(8,128)(2,1)}, u32[]{:S(2)}, u32[]{:S(2)}) async-start(bf16[4,128,768]{1,2,0:T(8,128)(2,1)} %copy.77), calls=%async_computation.3 | async-start | bytes 1572864 | tf_op jit(solution)/shard_map/all_to_all | solution.py:103
  237.0 23.7 %all-to-all-start.4 = ((bf16[4,128,768]{1,2,0:T(8,128)(2,1)}), bf16[4,128,768]{1,2,0:T(8,128)(2,1)}, u32[]{:S(2)}, u32[]{:S(2)}) async-start(bf16[4,128,768]{1,2,0:T(8,128)(2,1)} %copy.79), calls=%async_computation.4 | async-start | bytes 1572864 | tf_op jit(solution)/shard_map/all_to_all | solution.py:106
  260.7 23.2 %all-to-all-start.5 = ((bf16[4,128,768]{1,2,0:T(8,128)(2,1)}), bf16[4,128,768]{1,2,0:T(8,128)(2,1)S(1)}, u32[]{:S(2)}, u32[]{:S(2)}) async-start(bf16[4,128,768]{1,2,0:T(8,128)(2,1)} %copy.81), calls=%async_computation.5 | async-start | bytes 1572864 | tf_op jit(solution)/shard_map/all_to_all | solution.py:109
  285.1 49.9 %copy-start.3 = (bf16[768,768]{1,0:T(8,128)(2,1)S(1)}, bf16[768,768]{1,0:T(8,128)(2,1)}, u32[]{:S(2)}) copy-start(bf16[768,768]{1,0:T(8,128)(2,1)} %reduce-scatter.2.cloned.1.call-done) | copy-start | bytes 3538948
Sparse Core Ops, SparseCore 0:
  9.6 157.0 all-gather.2
  176.3 78.6 reduce-scatter.1
where the time goes:
time: 346 us; the launch traced here: 345 us
  waiting for transfers between devices  140 us (40%)
  matrix products  51.8 us (15%)
  blocking collectives  43.1 us (12%)
  starting transfers between devices  40 us (12%)
  local copies, waits for them, and re-layouts  34.8 us (10%)
  other arithmetic  17.4 us (5%)
  between operations  17.4 us (5%)
    psum x1, blocking collectives, local(): weight_squares = lax.psum(local_squares, ('dp', 'seq'))  43.1 us
    all_to_all x1, waiting for transfers between devices, local(): lax.all_to_all(key_rows[0], 'seq', split_axis=1, concat_axis=0, tiled=True)  36.6 us
    all_to_all x1, waiting for transfers between devices, local(): lax.all_to_all(query_rows[0], 'seq', split_axis=1, concat_axis=0, tiled=T...  34.2 us
    all_to_all x1, waiting for transfers between devices, local(): lax.all_to_all(value_rows[0], 'seq', split_axis=1, concat_axis=0, tiled=T...  31.4 us
    all_gather x1, waiting for transfers between devices, local(): out_full = lax.all_gather(out_grad[0], 'seq', axis=0, tiled=True)  14.7 us
    all_to_all x1, waiting for transfers between devices, local(): lax.all_to_all(value_grad.reshape(total, width), 'seq', split_axis=0, con...  11.8 us
    dot_general x1, matrix products, local(): jnp.dot(out_full, out_weight.T, preferred_element_type=jnp.float32)  10.7 us
    all_to_all x1, waiting for transfers between devices, local(): lax.all_to_all(key_grad.reshape(total, width), 'seq', split_axis=0, conca...  10.6 us
  transfers between devices with their start and end apart: 8, of which 6 were waited for; matrix products, arithmetic and copies ran while one was open for 23% of the time, Pallas kernels for 0%

commit v1 on v0

v1 whole, which is shorter than its diff:
```python
import functools
import jax
import jax.numpy as jnp
from jax import lax
from jax.experimental import pallas as pl
from jax.experimental.pallas import tpu as pltpu
from jax.sharding import PartitionSpec as P

HEAD_DIM = 128
MAX_NORM = 768
EPS = 1e-06
CORES = 2
CHUNKS = 3
HALVES = 2
LOADS = 1
TOGETHER = 3
VMEM_BYTES = 40 * 1024 * 1024


ANY = pl.BlockSpec(memory_space=pl.ANY)
SMEM = pl.BlockSpec(memory_space=pltpu.SMEM)
VMEM = pl.BlockSpec(memory_space=pltpu.VMEM)


def run(body, outs, args, in_specs, out_specs, scratch=(), grid=None):
    return pl.pallas_call(
        body,
        out_shape=outs,
        grid=() if grid is None else grid,
        in_specs=in_specs,
        out_specs=out_specs,
        scratch_shapes=list(scratch),
        compiler_params=pltpu.CompilerParams(vmem_limit_bytes=VMEM_BYTES),
    )(*args)


def chunk_count(heads):
    return max(c for c in range(1, CHUNKS + 1) if heads % c == 0)


def dot(a, b, dims=(1, 0)):
    contract = (((dims[0],), (dims[1],)), ((), ()))
    return lax.dot_general(a, b, contract, preferred_element_type=jnp.float32)


def pack_body(place_ref, *refs, ways, width):
    rows, outs = refs[:3], refs[3:]
    place = place_ref[0]
    for step in range(ways):
        column = pl.multiple_of(lax.rem(place + step, ways) * width, 128)
        for which in range(3):
            outs[step][which] = rows[which][:, pl.ds(column, width)]


def unpack_body(place_ref, *refs, ways, width, size):
    pieces, outs = refs[:-3], refs[-3:]
    place = place_ref[0]
    for slot, piece in enumerate(pieces):
        start, step = slot // ways * size, slot % ways
        column = pl.multiple_of(lax.rem(place + step, ways) * width + start, 128)
        for which in range(3):
            outs[which][:, pl.ds(column, size)] = piece[which]


def item_of(place, index, ways):
    both = jnp.minimum(place, ways - 1 - place)
    paired = index <= 2 * both
    hops = jnp.where(paired, (index + 1) // 2, index - both)
    lefty = jnp.where(paired, index % 2 == 1, 2 * place > ways - 1)
    return hops, lefty


def slot_of(place, index, ways):
    if index == 0:
        return jnp.int32(0)
    hops, lefty = item_of(place, index, ways)
    return jnp.where(lefty, hops, ways - hops)


def d_attn_body(place_ref, *refs, index, ways, groups, hops_list, rows, cols, aligned):
    pieces = HALVES if index == 0 else 2 * HALVES * len(hops_list)
    sources = refs[:pieces]
    weight = refs[pieces]
    outs = refs[pieces + 1 : -4]
    full, weight_vmem, sems, out_sems = refs[-4:]
    place = place_ref[0]
    group = place_ref[1]
    part = rows // HALVES
    depth = weight.shape[1] // LOADS
    loads = []
    for i in range(LOADS):
        at = pl.ds(i * depth, depth)
        loads.append(
            pltpu.make_async_copy(
                weight.at[:, at], weight_vmem.at[:, at], sems.at[HALVES + i]
            )
        )

    def fetch(first):
        return [
            pltpu.make_async_copy(
                sources[first + half], full.at[pl.ds(half * part, part)], sems.at[half]
            )
            for half in range(HALVES)
        ]

    def begin(first):
        for copy in fetch(first):
            copy.start()

    if index == 0:
        begin(0)
    else:
        hops, lefty = item_of(place, index, ways)
        for i, dist in enumerate(hops_list):
            for side in range(2):
                here = jnp.logical_and(hops == dist, lefty == (side == 0))

                @pl.when(here)
                def _(first=(2 * i + side) * HALVES):
                    begin(first)

    for load in loads:
        load.start()
    for copy in fetch(0):
        copy.wait()
    writes = []
    if aligned:
        for mask in range(groups):
            column = pl.multiple_of(lax.bitwise_xor(group, mask) * cols, 128)
            writes.append(
                pltpu.make_async_copy(
                    full.at[:, pl.ds(column, cols)], outs[1 + mask], out_sems.at[mask]
                )
            )
    else:
        writes.append(pltpu.make_async_copy(full, outs[1], out_sems.at[0]))
    for write in writes:
        write.start()
    total = None
    for i, load in enumerate(loads):
        load.wait()
        at = slice(i * depth, (i + 1) * depth)
        term = dot(full[:, at], weight_vmem[:, at], (1, 1))
        total = term if total is None else total + term
    outs[0][...] = total.astype(jnp.bfloat16)
    for write in writes:
        write.wait()


def segments(place, lengths_ref, shape, dim, ways, rows):
    index = lax.broadcasted_iota(jnp.int32, shape, dim)
    source = place - lax.div(index, rows)
    source = jnp.where(source < 0, source + ways, source)
    position = source * rows + lax.rem(index, rows)
    seg = jnp.zeros(shape, jnp.int32)
    end = jnp.int32(0)
    for clip in range(lengths_ref.shape[1]):
        end = end + lengths_ref[0, clip]
        seg = seg + (position >= end).astype(jnp.int32)
    return seg


def norm_rows(raw, gain):
    wide = raw.astype(jnp.float32)
    inverse = lax.rsqrt(jnp.mean(wide * wide, axis=-1, keepdims=True) + EPS)
    unit = wide * inverse
    return unit, inverse, (unit * gain).astype(jnp.bfloat16)


def norm_back(unit, inverse, gain, d_norm):
    d_unit = d_norm * gain
    grad = inverse * (d_unit - unit * jnp.mean(unit * d_unit, axis=-1, keepdims=True))
    return grad.astype(jnp.bfloat16), jnp.sum(unit * d_norm, axis=0, keepdims=True)


def forward_body(place_ref, lengths_ref, *refs, ways, rows):
    pieces = refs[:ways]
    q_gain_ref, k_gain_ref, attn_t_ref, probs_ref = refs[ways:]
    total = ways * rows
    place = place_ref[0]
    scale = HEAD_DIM ** (-0.5)
    same = segments(place, lengths_ref, (total, 1), 0, ways, rows) == segments(
        place, lengths_ref, (1, total), 1, ways, rows
    )

    def gather(which):
        return jnp.concatenate([piece[which] for piece in pieces], axis=0)

    _, _, q_norm = norm_rows(gather(0), q_gain_ref[...])
    _, _, k_norm = norm_rows(gather(1), k_gain_ref[...])
    value = gather(2)
    scores = dot(k_norm, q_norm, (1, 1)) * scale
    expo = jnp.where(same, jnp.exp(scores), 0.0)
    inverse_sum = 1.0 / jnp.sum(expo, axis=0, keepdims=True)
    probs = (expo * inverse_sum).astype(jnp.bfloat16)
    probs_ref[0] = probs
    attn_t_ref[...] = dot(value.T, probs).astype(jnp.bfloat16)


def backward_body(place_ref, *refs, ways, rows, heads):
    pieces = refs[:ways]
    d_pieces = refs[ways : 2 * ways]
    probs_ref, q_gain_ref, k_gain_ref, gains_ref = refs[2 * ways : 2 * ways + 4]
    outs = refs[2 * ways + 4 : 3 * ways + 4]
    d_attn_ref = refs[-1]
    place = place_ref[0]
    scale = HEAD_DIM ** (-0.5)
    for index in range(ways):
        row = pl.multiple_of(slot_of(place, index, ways) * rows, rows)
        d_attn_ref[pl.ds(row, rows), :] = d_pieces[index][...]
    q_gain = q_gain_ref[...]
    k_gain = k_gain_ref[...]
    q_sum = jnp.zeros((1, HEAD_DIM), jnp.float32)
    k_sum = jnp.zeros((1, HEAD_DIM), jnp.float32)
    for head in range(heads):
        part = slice(head * HEAD_DIM, (head + 1) * HEAD_DIM)

        def gather(which):
            return jnp.concatenate([piece[which, :, part] for piece in pieces], axis=0)

        q_unit, q_inv, q_norm = norm_rows(gather(0), q_gain)
        k_unit, k_inv, k_norm = norm_rows(gather(1), k_gain)
        value = gather(2)
        d_attn = d_attn_ref[:, part]
        probs = probs_ref[head]
        d_probs = dot(value, d_attn, (1, 1))
        probs32 = probs.astype(jnp.float32)
        row_sum = jnp.sum(probs32 * d_probs, axis=0, keepdims=True)
        d_scores = (probs32 * (d_probs - row_sum) * scale).astype(jnp.bfloat16)
        d_value = dot(probs, d_attn).astype(jnp.bfloat16)
        d_k = dot(d_scores, q_norm)
        d_q = dot(k_norm.T, d_scores).T
        q_grad, q_part = norm_back(q_unit, q_inv, q_gain, d_q)
        k_grad, k_part = norm_back(k_unit, k_inv, k_gain, d_k)
        q_sum = q_sum + q_part
        k_sum = k_sum + k_part
        for step in range(ways):
            block = slice(step * rows, (step + 1) * rows)
            outs[step][0, :, part] = q_grad[block]
            outs[step][1, :, part] = k_grad[block]
            outs[step][2, :, part] = d_value[block]
    gains_ref[...] = jnp.concatenate(
        [q_sum, k_sum, jnp.zeros((6, HEAD_DIM), jnp.float32)], axis=0
    )


def weight_body(place_ref, *refs, items, ways, groups, rows, first, last):
    attn = refs[:groups]
    columns = refs[groups : (1 + len(items)) * groups]
    out = refs[(1 + len(items)) * groups + (0 if first else 1)]
    left, right, before, sems, before_sem = refs[-5:]
    if not first:
        fetch = pltpu.make_async_copy(refs[(1 + len(items)) * groups], before, before_sem)
        fetch.start()
    copies = []
    for i, index in enumerate(items):
        slot = pl.multiple_of(slot_of(place_ref[0], index, ways) * rows, 128)
        copies.append([])
        for mask in range(groups):
            at = pl.ds(mask * rows, rows)
            source = attn[mask].at[:, pl.ds(slot, rows)]
            copies[-1].append(
                pltpu.make_async_copy(source, left.at[i, :, at], sems.at[i, 2 * mask])
            )
            source = columns[i * groups + mask]
            copies[-1].append(
                pltpu.make_async_copy(source, right.at[i, at], sems.at[i, 2 * mask + 1])
            )
    for group in copies:
        for copy in group:
            copy.start()
    total = None
    for i, group in enumerate(copies):
        for copy in group:
            copy.wait()
        term = dot(left[i], right[i])
        total = term if total is None else total + term
    if not first:
        fetch.wait()
        total = total + before[...]
    out[...] = total
    if last:
        refs[(1 + len(items)) * groups + 2][...] = jnp.sum(total * total, axis=0, keepdims=True)


def weight_items(ways):
    count = ways - 1
    starts = range(0, count, TOGETHER)
    return [list(range(i, min(i + TOGETHER, count))) for i in starts] + [[count]]


def make_local(groups, ways):
    def local(
        query_rows, key_rows, value_rows, out_grad, clip_lengths, out_weight, query_gain, key_gain
    ):
        place = lax.axis_index("seq")
        group = lax.axis_index("dp")
        places = jnp.stack([place, group]).astype(jnp.int32)
        rows, features = query_rows.shape[1:]
        width = features // ways
        heads = width // HEAD_DIM
        count = chunk_count(heads)
        size = width // count
        model = out_grad.shape[2]
        cols = model // groups
        aligned = cols % 128 == 0
        total = ways * rows
        bf16 = jnp.bfloat16
        f32 = jnp.float32
        barrier = lax.optimization_barrier

        def struct(*shape, dtype=bf16):
            return jax.ShapeDtypeStruct(shape, dtype)

        def shift(x, step):
            return lax.ppermute(x, "seq", [(i, (i + step) % ways) for i in range(ways)])

        def partner(x, mask):
            return lax.ppermute(x, "dp", [(i, i ^ mask) for i in range(groups)])

        packed = run(
            functools.partial(pack_body, ways=ways, width=width),
            [struct(3, rows, width)] * ways,
            (places, query_rows[0], key_rows[0], value_rows[0]),
            [SMEM, VMEM, VMEM, VMEM],
            [VMEM] * ways,
        )
        pieces = [packed[0]] + [shift(packed[step], step) for step in range(1, ways)]

        extra = [struct(rows, cols)] * groups if aligned else [struct(rows, model)]
        part = rows // HALVES
        own = [out_grad[0, half * part : (half + 1) * part] for half in range(HALVES)]
        right, left = [own], [own]
        d_attn, columns = [], []
        for index in range(ways):
            if index > 0:
                up = [(i, i + 1) for i in range(index - 1, ways - 1)]
                down = [(i, i - 1) for i in range(1, ways - index + 1)]
                right.append([])
                left.append([])
                for half in range(HALVES):
                    right[-1].append(lax.ppermute(right[-2][half], "seq", up))
                    left[-1].append(lax.ppermute(left[-2][half], "seq", down))
            hops_list = list(range((index + 1) // 2, index + 1)) if index else []
            sources = [x for dist in hops_list for side in (right, left) for x in side[dist]] or own
            results = run(
                functools.partial(
                    d_attn_body,
                    index=index,
                    ways=ways,
                    groups=groups,
                    hops_list=hops_list,
                    rows=rows,
                    cols=cols,
                    aligned=aligned,
                ),
                [struct(rows, width)] + extra,
                (places, *sources, out_weight),
                [SMEM] + [ANY] * (len(sources) + 1),
                [VMEM] + [ANY] * len(extra),
                [
                    pltpu.VMEM((rows, model), bf16),
                    pltpu.VMEM(out_weight.shape, bf16),
                    pltpu.SemaphoreType.DMA((HALVES + LOADS,)),
                    pltpu.SemaphoreType.DMA((groups,)),
                ],
            )
            d_attn.append(results[0])
            blocks = results[1:]
            if not aligned:
                blocks = [
                    lax.dynamic_slice_in_dim(results[1], (group ^ mask) * cols, cols, 1)
                    for mask in range(groups)
                ]
            got = {mask: partner(blocks[mask], mask) for mask in reversed(range(1, groups))}
            columns.append([blocks[0]] + [got[mask] for mask in range(1, groups)])

        attn_t, probs = run(
            functools.partial(forward_body, ways=ways, rows=rows),
            [struct(width, total), struct(heads, total, total)],
            (places, clip_lengths, *pieces, query_gain[None], key_gain[None]),
            [SMEM, SMEM]
            + [pl.BlockSpec((3, rows, HEAD_DIM), lambda h: (0, 0, h))] * ways
            + [pl.BlockSpec((1, HEAD_DIM), lambda h: (0, 0))] * 2,
            [
                pl.BlockSpec((HEAD_DIM, total), lambda h: (h, 0)),
                pl.BlockSpec((1, total, total), lambda h: (h, 0, 0)),
            ],
            grid=(heads,),
        )
        attn = [attn_t]
        for mask in range(1, groups):
            if mask % CORES:
                attn.append(partner(attn[mask - 1], 1))
            else:
                attn.append(partner(attn_t, mask))

        gains = 0.0
        back = []
        for index in range(count):
            results = run(
                functools.partial(
                    backward_body, ways=ways, rows=rows, heads=size // HEAD_DIM
                ),
                [struct(8, HEAD_DIM, dtype=f32)] + [struct(3, rows, size)] * ways,
                (places, *pieces, *d_attn, probs, query_gain[None], key_gain[None]),
                [SMEM]
                + [pl.BlockSpec((3, rows, size), lambda i, at=index: (0, 0, at))] * ways
                + [pl.BlockSpec((rows, size), lambda i, at=index: (0, at))] * ways
                + [pl.BlockSpec((size // HEAD_DIM, total, total), lambda i, at=index: (at, 0, 0))]
                + [pl.BlockSpec((1, HEAD_DIM), lambda i: (0, 0))] * 2,
                [pl.BlockSpec((8, HEAD_DIM), lambda i: (0, 0))]
                + [pl.BlockSpec((3, rows, size), lambda i: (0, 0, 0))] * ways,
                [pltpu.VMEM((total, size), bf16)],
                grid=(1,),
            )
            gains = gains + results[0]
            grads = results[1:]
            back.extend([grads[0]] + [shift(grads[step], -step) for step in range(1, ways)])

        weight_raw = None
        for items in weight_items(ways):
            first, last = weight_raw is None, items[-1] == ways - 1
            results = run(
                functools.partial(
                    weight_body,
                    items=items,
                    ways=ways,
                    groups=groups,
                    rows=rows,
                    first=first,
                    last=last,
                ),
                [struct(width, cols, dtype=f32)]
                + ([struct(1, cols, dtype=f32)] if last else []),
                (places, *attn)
                + tuple(x for index in items for x in columns[index])
                + (() if first else (weight_raw,)),
                [SMEM] + [ANY] * ((1 + len(items)) * groups + (0 if first else 1)),
                [VMEM] * (2 if last else 1),
                [
                    pltpu.VMEM((len(items), width, groups * rows), bf16),
                    pltpu.VMEM((len(items), groups * rows, cols), bf16),
                    pltpu.VMEM((width, cols), f32),
                    pltpu.SemaphoreType.DMA((len(items), 2 * groups)),
                    pltpu.SemaphoreType.DMA,
                ],
            )
            weight_raw = results[0]

        squares = jnp.sum(results[1])
        row = lax.broadcasted_iota(jnp.int32, gains.shape, 0)
        sent = jnp.where(row == 2, squares / HEAD_DIM, gains)
        mask = 1
        while mask < groups:
            sent = sent + partner(sent, mask)
            mask *= 2
        mask = 1
        while mask < ways:
            sent = sent + lax.ppermute(sent, "seq", [(i, i ^ mask) for i in range(ways)])
            mask *= 2
        qgain_raw, kgain_raw = sent[0], sent[1]
        grad_norm = jnp.sqrt(
            jnp.sum(sent[2]) + jnp.sum(qgain_raw * qgain_raw) + jnp.sum(kgain_raw * kgain_raw)
        )
        factor = jnp.minimum(jnp.float32(1.0), MAX_NORM / (grad_norm + EPS))
        weight_grad = weight_raw * factor
        tail = back[-ways + 1 :]
        tail, weight_grad = barrier((tail, weight_grad))
        back = back[: -ways + 1] + tail
        outs = run(
            functools.partial(unpack_body, ways=ways, width=width, size=size),
            [struct(rows, features)] * 3,
            (places, *back),
            [SMEM] + [VMEM] * len(back),
            [VMEM] * 3,
        )

        return (
            outs[0][None],
            outs[1][None],
            outs[2][None],
            weight_grad,
            qgain_raw * factor,
            kgain_raw * factor,
            grad_norm,
        )

    return local


def solution(mesh):
    rows = P("dp", "seq", None)
    groups, ways = mesh.shape["dp"], mesh.shape["seq"]
    body = make_local(groups, ways)

    return jax.shard_map(
        body,
        mesh=mesh,
        in_specs=(rows, rows, rows, rows, P("dp", None), P("seq", None), P(), P()),
        out_specs=(rows, rows, rows, P("seq", "dp"), P(), P(), P()),
        check_vma=False,
    )
```

time: 346 us -> 359 us (1.038)
  Pallas kernels: 0 us -> 62.6 us
  matrix products: 51.8 us -> 0 us
  blocking collectives: 43.1 us -> 0 us
  starting transfers between devices: 40 us -> 80.3 us
  waiting for transfers between devices: 140 us -> 167 us
  other arithmetic: 17.4 us -> 5.24 us
  between operations: 17.4 us -> 5.35 us
    ppermute x0 -> x64, waiting for transfers between devices: none -> 167 us  [the longest x6 73.5 us: local(): left[-1].append(lax.ppermute(left[-2][half], 'seq', down))]
    all_to_all x6 -> x0, waiting for transfers between devices: 125 us -> none  [the longest x1 36.6 us: local(): lax.all_to_all(key_rows[0], 'seq', split_axis=1, concat_axis=0, tiled=True)]
    ppermute x0 -> x64, starting transfers between devices: none -> 80.3 us  [the longest x38 31.5 us: partner(): return lax.ppermute(x, 'dp', [(i, i ^ mask) for i in range(groups)])]
    pallas_call x0 -> x12, Pallas kernels: none -> 62.6 us  [run(): pl.pallas_call(body, out_shape=outs, grid=() if grid is None else grid, i...]
    dot_general x8 -> x0, matrix products: 51.8 us -> none  [the longest x1 10.7 us: local(): jnp.dot(out_full, out_weight.T, preferred_element_type=jnp.float32)]
    psum x1 -> x0, blocking collectives: 43.1 us -> none  [local(): weight_squares = lax.psum(local_squares, ('dp', 'seq'))]
    all_to_all x6 -> x0, starting transfers between devices: 40 us -> none  [the longest x1 8.03 us: local(): lax.all_to_all(key_rows[0], 'seq', split_axis=1, concat_axis=0, tiled=True)]
    unnamed x28 -> x158, local copies, waits for them, and re-layouts: 9.85 us -> 31.4 us
  transfers between devices with their start and end apart: 8 -> 64, of which waited for: 6 -> 27; matrix products, arithmetic and copies ran while one was open for 23% -> 1% of each run, Pallas kernels for 0% -> 16%
where the time goes in v1:
time: 359 us; the launch traced here: 354 us
  waiting for transfers between devices  167 us (47%)
  starting transfers between devices  80.3 us (22%)
  Pallas kernels  62.6 us (17%)
  local copies, waits for them, and re-layouts  34 us (9%)
  between operations  5.35 us (1%)
  other arithmetic  5.24 us (1%)
    ppermute x6, waiting for transfers between devices, local(): left[-1].append(lax.ppermute(left[-2][half], 'seq', down))  73.5 us
    pallas_call x12, Pallas kernels, run(): pl.pallas_call(body, out_shape=outs, grid=() if grid is None else grid, i...  62.6 us
    ppermute x12, waiting for transfers between devices, shift(): return lax.ppermute(x, 'seq', [(i, (i + step) % ways) for i in range(ways)])  41.8 us
    ppermute x38, waiting for transfers between devices, partner(): return lax.ppermute(x, 'dp', [(i, i ^ mask) for i in range(groups)])  39.5 us
    ppermute x38, starting transfers between devices, partner(): return lax.ppermute(x, 'dp', [(i, i ^ mask) for i in range(groups)])  31.5 us
    unnamed x158, local copies, waits for them, and re-layouts  31.4 us
    ppermute x12, starting transfers between devices, shift(): return lax.ppermute(x, 'seq', [(i, (i + step) % ways) for i in range(ways)])  21.3 us
    ppermute x6, starting transfers between devices, local(): left[-1].append(lax.ppermute(left[-2][half], 'seq', down))  13.3 us
  transfers between devices with their start and end apart: 64, of which 27 were waited for; matrix products, arithmetic and copies ran while one was open for 1% of the time, Pallas kernels for 16%

profile of v1, /device:TPU:12, one launch (start us, length us, event | category | flops | bytes accessed | tf_op | source)
XLA Modules:
  0.0 354.1 jit_solution(47112031783485521)
XLA Ops:
  6.8 3.5 collective-permute-start.4
  13.6 3.7 %copy-done = bf16[768,6144]{1,0:T(8,128)(2,1)S(1)} copy-done((bf16[768,6144]{1,0:T(8,128)(2,1)S(1)}, bf16[768,6144]{1,0:T(8,128)(2,1)}, u32[]{:S(2)}) %copy-start) | copy-done | bytes 9437208
  17.2 5.7 %shard_map.136 = (bf16[128,768]{1,0:T(8,128)(2,1)S(1)}, bf16[128,768]{1,0:T(8,128)(2,1)S(1)}, bf16[128,768]{1,0:T(8,128)(2,1)S(1)}, bf16[128,768]{1,0:T(8,128)(2...) custom-call(s32[2]{0:T(128)S(1)} %pad_add_fusion.place_ref, ...), custom_call_target="tpu_custom_call" | custom-call | tf_op jit(solution)/shard_map/pallas_call | solution.py:26
  30.3 4.0 %collective-permute-done.39.refs_10_ = bf16[128,768]{1,0:T(8,128)(2,1)S(1)} collective-permute-done((bf16[128,768]{1,0:T(8,128)(2,1)S(1)}, bf16[128,768]{1,0:T(8,128)(2,1)S(1)}, u32[]{:S(2)}, u32[]{:S(2)}) %collective-permute-start.39) | collective-permute-done | bytes 196640 | tf_op jit(solution)/shard_map/ppermute | solution.py:320
  36.2 6.5 %collective-permute-done.4.refs_1_ = bf16[64,6144]{1,0:T(8,128)(2,1)} collective-permute-done((bf16[64,6144]{1,0:T(8,128)(2,1)}, bf16[64,6144]{1,0:T(8,128)(2,1)}, u32[]{:S(2)}, u32[]{:S(2)}) %collective-permute-start.4) | collective-permute-done | bytes 786464 | tf_op jit(solution)/shard_map/ppermute | solution.py:343
  42.8 31.3 %collective-permute-done.6.refs_3_ = bf16[64,6144]{1,0:T(8,128)(2,1)S(1)} collective-permute-done((bf16[64,6144]{1,0:T(8,128)(2,1)}, bf16[64,6144]{1,0:T(8,128)(2,1)S(1)}, u32[]{:S(2)}, u32[]{:S(2)}) %collective-permute-start.6) | collective-permute-done | bytes 786464 | tf_op jit(solution)/shard_map/ppermute | solution.py:344
  74.8 5.4 %shard_map.137 = (bf16[128,768]{1,0:T(8,128)(2,1)S(1)}, bf16[128,768]{1,0:T(8,128)(2,1)S(1)}, bf16[128,768]{1,0:T(8,128)(2,1)S(1)}, bf16[128,768]{1,0:T(8,128)(2...) custom-call(s32[2]{0:T(128)S(1)} %pad_add_fusion.place_ref, ...), custom_call_target="tpu_custom_call" | custom-call | tf_op jit(solution)/shard_map/pallas_call | solution.py:26
  82.9 8.3 %collective-permute-done.1.refs_2_ = bf16[3,128,768]{2,1,0:T(8,128)(2,1)S(1)} collective-permute-done((bf16[3,128,768]{2,1,0:T(8,128)(2,1)S(1)}, bf16[3,128,768]{2,1,0:T(8,128)(2,1)S(1)}, u32[]{:S(2)}, u32[]{:S(2)}) %collective-permute-start.1) | collective-permute-done | bytes 589856 | tf_op jit(solution)/shard_map/ppermute | solution.py:317
  91.2 7.3 %collective-permute-done.2.refs_3_ = bf16[3,128,768]{2,1,0:T(8,128)(2,1)S(1)} collective-permute-done((bf16[3,128,768]{2,1,0:T(8,128)(2,1)S(1)}, bf16[3,128,768]{2,1,0:T(8,128)(2,1)S(1)}, u32[]{:S(2)}, u32[]{:S(2)}) %collective-permute-start.2) | collective-permute-done | bytes 589856 | tf_op jit(solution)/shard_map/ppermute | solution.py:317
  98.5 6.8 %shard_map.140 = (bf16[768,512]{1,0:T(8,128)(2,1)S(1)}, bf16[6,512,512]{2,1,0:T(8,128)(2,1)S(1)}) custom-call(s32[2]{0:T(128)S(1)} %pad_add_fusion.place_ref, s32[1,4]{1,0:T(1,128)S(1)} %copy-done.56, bf16[3,128,768]{2,1,0:T(8,128)(2,1)S(1)} %get-tuple-element.73.refs_0_, bf16[3,128,768]{2,1,0:T(8,128)(2,1)S(1)} %collective-permute-done.refs_1_, ...), custom_call_target="tpu_custom_call" | custom-call | tf_op jit(solution)/shard_map/pallas_call | solution.py:26
  122.2 5.8 %collective-permute-done.49.refs_21_ = bf16[128,768]{1,0:T(8,128)(2,1)S(1)} collective-permute-done((bf16[128,768]{1,0:T(8,128)(2,1)S(1)}, bf16[128,768]{1,0:T(8,128)(2,1)S(1)}, u32[]{:S(2)}, u32[]{:S(2)}) %collective-permute-start.49) | collective-permute-done | bytes 196640 | tf_op jit(solution)/shard_map/ppermute | solution.py:320
  140.9 3.6 %collective-permute-done.8.refs_5_.refs_1_ = bf16[64,6144]{1,0:T(8,128)(2,1)S(1)} collective-permute-done((bf16[64,6144]{1,0:T(8,128)(2,1)}, bf16[64,6144]{1,0:T(8,128)(2,1)S(1)}, u32[]{:S(2)}, u32[]{:S(2)}) %collective-permute-start.8) | collective-permute-done | bytes 786464 | tf_op jit(solution)/shard_map/ppermute | solution.py:343
  145.9 7.8 %collective-permute-done.9.refs_6_.refs_2_ = bf16[64,6144]{1,0:T(8,128)(2,1)S(1)} collective-permute-done((bf16[64,6144]{1,0:T(8,128)(2,1)}, bf16[64,6144]{1,0:T(8,128)(2,1)S(1)}, u32[]{:S(2)}, u32[]{:S(2)}) %collective-permute-start.9) | collective-permute-done | bytes 786464 | tf_op jit(solution)/shard_map/ppermute | solution.py:344
  154.5 15.1 %collective-permute-done.10.refs_7_.refs_3_ = bf16[64,6144]{1,0:T(8,128)(2,1)S(1)} collective-permute-done((bf16[64,6144]{1,0:T(8,128)(2,1)S(1)}, bf16[64,6144]{1,0:T(8,128)(2,1)S(1)}, u32[]{:S(2)}, u32[]{:S(2)}) %collective-permute-start.10) | collective-permute-done | bytes 786464 | tf_op jit(solution)/shard_map/ppermute | solution.py:344
  170.3 7.8 %shard_map.138 = (bf16[128,768]{1,0:T(8,128)(2,1)S(1)}, bf16[128,768]{1,0:T(8,128)(2,1)S(1)}, bf16[128,768]{1,0:T(8,128)(2,1)S(1)}, bf16[128,768]{1,0:T(8,128)(2...) custom-call(s32[2]{0:T(128)S(1)} %pad_add_fusion.place_ref, ...), custom_call_target="tpu_custom_call" | custom-call | tf_op jit(solution)/shard_map/pallas_call | solution.py:26
  182.0 4.7 %collective-permute-done.53.refs_26_ = bf16[128,768]{1,0:T(8,128)(2,1)S(1)} collective-permute-done((bf16[128,768]{1,0:T(8,128)(2,1)S(1)}, bf16[128,768]{1,0:T(8,128)(2,1)S(1)}, u32[]{:S(2)}, u32[]{:S(2)}) %collective-permute-start.53) | collective-permute-done | bytes 196640 | tf_op jit(solution)/shard_map/ppermute | solution.py:320
  193.7 6.0 %collective-permute-done.56.refs_29_ = bf16[128,768]{1,0:T(8,128)(2,1)S(1)} collective-permute-done((bf16[128,768]{1,0:T(8,128)(2,1)S(1)}, bf16[128,768]{1,0:T(8,128)(2,1)S(1)}, u32[]{:S(2)}, u32[]{:S(2)}) %collective-permute-start.56) | collective-permute-done | bytes 196640 | tf_op jit(solution)/shard_map/ppermute | solution.py:320
  201.0 5.6 %collective-permute-done.13.refs_6_ = bf16[64,6144]{1,0:T(8,128)(2,1)S(1)} collective-permute-done((bf16[64,6144]{1,0:T(8,128)(2,1)S(1)}, bf16[64,6144]{1,0:T(8,128)(2,1)S(1)}, u32[]{:S(2)}, u32[]{:S(2)}) %collective-permute-start.13) | collective-permute-done | bytes 786464 | tf_op jit(solution)/shard_map/ppermute | solution.py:344
  207.9 13.7 %collective-permute-done.14.refs_7_ = bf16[64,6144]{1,0:T(8,128)(2,1)S(1)} collective-permute-done((bf16[64,6144]{1,0:T(8,128)(2,1)S(1)}, bf16[64,6144]{1,0:T(8,128)(2,1)S(1)}, u32[]{:S(2)}, u32[]{:S(2)}) %collective-permute-start.14) | collective-permute-done | bytes 786464 | tf_op jit(solution)/shard_map/ppermute | solution.py:344
  221.6 7.9 %shard_map.139 = (bf16[128,768]{1,0:T(8,128)(2,1)S(1)}, bf16[128,768]{1,0:T(8,128)(2,1)S(1)}, bf16[128,768]{1,0:T(8,128)(2,1)S(1)}, bf16[128,768]{1,0:T(8,128)(2...) custom-call(s32[2]{0:T(128)S(1)} %pad_add_fusion.place_ref, ...), custom_call_target="tpu_custom_call" | custom-call | tf_op jit(solution)/shard_map/pallas_call | solution.py:26
  252.2 13.9 %shard_map.144.refs_16_ = f32[768,768]{1,0:T(8,128)S(1)} custom-call(s32[2]{0:T(128)S(1)} %pad_add_fusion.place_ref, bf16[768,512]{1,0:T(8,128)(2,1)S(1)} %get-tuple-element.94.refs_0_, bf16[768,512]{1,0:T(8,128)(2,1)S(1)} %collective-permute-done.24.refs_1_, bf16[768,512]{1,0:T(8,128)(2,1)S(1)} %collective-permute-done.25.refs_2_, ...), custom_call_target="tpu_custom_call" | custom-call | tf_op jit(solution)/shard_map/pallas_call | solution.py:26
  277.0 4.9 %shard_map.145 = (f32[768,768]{1,0:T(8,128)S(1)}, f32[1,768]{1,0:T(1,128)S(1)}) custom-call(s32[2]{0:T(128)S(1)} %pad_add_fusion.place_ref, bf16[768,512]{1,0:T(8,128)(2,1)S(1)} %get-tuple-element.94.refs_0_, bf16[768,512]{1,0:T(8,128)(2,1)S(1)} %collective-permute-done.24.refs_1_, bf16[768,512]{1,0:T(8,128)(2,1)S(1)} %collective-permute-done.25.refs_2_, ...), custom_call_target="tpu_custom_call" | custom-call | tf_op jit(solution)/shard_map/pallas_call | solution.py:26
  312.6 19.3 %collective-permute-done.21.refs_9_ = bf16[3,128,256]{2,1,0:T(8,128)(2,1)S(1)} collective-permute-done((bf16[3,128,256]{2,1,0:T(8,128)(2,1)}, bf16[3,128,256]{2,1,0:T(8,128)(2,1)S(1)}, u32[]{:S(2)}, u32[]{:S(2)}) %collective-permute-start.21) | collective-permute-done | bytes 196640 | tf_op jit(solution)/shard_map/ppermute | solution.py:317
  331.9 9.9 %collective-permute-start.18 = (bf16[3,128,256]{2,1,0:T(8,128)(2,1)S(1)}, bf16[3,128,256]{2,1,0:T(8,128)(2,1)S(1)}, u32[]{:S(2)}, u32[]{:S(2)}) collective-permute-start(bf16[3,128,256]{2,1,0:T(8,128)(2,1)S(1)} %copy-done.64), channel_id=1, source_target_pairs={{0,3},{1,0},{2,1},{3,2},{4,7},{5,4},{6,5},{7,6},{8,11},{9,8},{10,9... | collective-permute-start | bytes 589832 | tf_op jit(solution)/shard_map/ppermute | solution.py:317
  (287 shorter events, 140.3 us)
Async XLA Ops:
  3.3 32.7 %collective-permute-start.3 = (bf16[64,6144]{1,0:T(8,128)(2,1)}, bf16[64,6144]{1,0:T(8,128)(2,1)}, u32[]{:S(2)}, u32[]{:S(2)}) collective-permute-start(bf16[64,6144]{1,0:T(8,128)(2,1)} %get-tuple-element.143.refs_0_), channel_id=1, source_target_pairs={{0,1},{1,2},{2,3},{4,5},{5,6},{6,7},{8,9},{9,10},{10,11},{12,13},{... | collective-permute-start | bytes 2359304 | tf_op jit(solution)/shard_map/ppermute | solution.py:343
  6.8 36.0 %collective-permute-start.4 = (bf16[64,6144]{1,0:T(8,128)(2,1)}, bf16[64,6144]{1,0:T(8,128)(2,1)}, u32[]{:S(2)}, u32[]{:S(2)}) collective-permute-start(bf16[64,6144]{1,0:T(8,128)(2,1)} %get-tuple-element.142.refs_1_), channel_id=1, source_target_pairs={{0,1},{1,2},{2,3},{4,5},{5,6},{6,7},{8,9},{9,10},{10,11},{12,13},{... | collective-permute-start | bytes 2359304 | tf_op jit(solution)/shard_map/ppermute | solution.py:343
  25.0 49.2 %collective-permute-start.6 = (bf16[64,6144]{1,0:T(8,128)(2,1)}, bf16[64,6144]{1,0:T(8,128)(2,1)S(1)}, u32[]{:S(2)}, u32[]{:S(2)}) collective-permute-start(bf16[64,6144]{1,0:T(8,128)(2,1)} %get-tuple-element.142.refs_1_), channel_id=1, source_target_pairs={{1,0},{2,1},{3,2},{5,4},{6,5},{7,6},{9,8},{10,9},{11,10},{13,12},{... | collective-permute-start | bytes 2359304 | tf_op jit(solution)/shard_map/ppermute | solution.py:344
  34.3 46.1 %collective-permute-start = (bf16[3,128,768]{2,1,0:T(8,128)(2,1)S(1)}, bf16[3,128,768]{2,1,0:T(8,128)(2,1)S(1)}, u32[]{:S(2)}, u32[]{:S(2)}) collective-permute-start(bf16[3,128,768]{2,1,0:T(8,128)(2,1)S(1)} %get-tuple-element.74), channel_id=1, source_target_pairs={{0,1},{1,2},{2,3},{3,0},{4,5},{5,6},{6,7},{7,4},{8,9},{9,10},{10,1... | collective-permute-start | bytes 1769480 | tf_op jit(solution)/shard_map/ppermute | solution.py:317
  36.0 55.2 %collective-permute-start.1 = (bf16[3,128,768]{2,1,0:T(8,128)(2,1)S(1)}, bf16[3,128,768]{2,1,0:T(8,128)(2,1)S(1)}, u32[]{:S(2)}, u32[]{:S(2)}) collective-permute-start(bf16[3,128,768]{2,1,0:T(8,128)(2,1)S(1)} %get-tuple-element.75), channel_id=1, source_target_pairs={{0,2},{1,3},{2,0},{3,1},{4,6},{5,7},{6,4},{7,5},{8,10},{9,11},{10,... | collective-permute-start | bytes 1769480 | tf_op jit(solution)/shard_map/ppermute | solution.py:317
  42.7 55.8 %collective-permute-start.2 = (bf16[3,128,768]{2,1,0:T(8,128)(2,1)S(1)}, bf16[3,128,768]{2,1,0:T(8,128)(2,1)S(1)}, u32[]{:S(2)}, u32[]{:S(2)}) collective-permute-start(bf16[3,128,768]{2,1,0:T(8,128)(2,1)S(1)} %get-tuple-element.76), channel_id=1, source_target_pairs={{0,3},{1,0},{2,1},{3,2},{4,7},{5,4},{6,5},{7,6},{8,11},{9,8},{10,9... | collective-permute-start | bytes 1769480 | tf_op jit(solution)/shard_map/ppermute | solution.py:317
  42.8 37.5 %collective-permute-start.40 = (bf16[128,768]{1,0:T(8,128)(2,1)S(1)}, bf16[128,768]{1,0:T(8,128)(2,1)S(1)}, u32[]{:S(2)}, u32[]{:S(2)}) collective-permute-start(bf16[128,768]{1,0:T(8,128)(2,1)S(1)} %copy-done.78), channel_id=1, source_target_pairs={{0,12},{4,8},{8,4},{12,0},{16,28},{20,24},{24,20},{28,16},{1,13},{... | collective-permute-start | bytes 589832 | tf_op jit(solution)/shard_map/ppermute | solution.py:320
  109.7 34.8 %collective-permute-start.8 = (bf16[64,6144]{1,0:T(8,128)(2,1)}, bf16[64,6144]{1,0:T(8,128)(2,1)S(1)}, u32[]{:S(2)}, u32[]{:S(2)}) collective-permute-start(bf16[64,6144]{1,0:T(8,128)(2,1)} %collective-permute-done.4.refs_1_), channel_id=1, source_target_pairs={{1,2},{2,3},{5,6},{6,7},{9,10},{10,11},{13,14},{14,15},{17,18},{18... | collective-permute-start | bytes 2359304 | tf_op jit(solution)/shard_map/ppermute | solution.py:343
  136.6 33.0 %collective-permute-start.10 = (bf16[64,6144]{1,0:T(8,128)(2,1)S(1)}, bf16[64,6144]{1,0:T(8,128)(2,1)S(1)}, u32[]{:S(2)}, u32[]{:S(2)}) collective-permute-start(bf16[64,6144]{1,0:T(8,128)(2,1)S(1)} %collective-permute-done.6.refs_3_), channel_id=1, source_target_pairs={{1,0},{2,1},{5,4},{6,5},{9,8},{10,9},{13,12},{14,13},{17,16},{18,1... | collective-permute-start | bytes 2359304 | tf_op jit(solution)/shard_map/ppermute | solution.py:344
  138.5 40.3 %collective-permute-start.25 = (bf16[768,512]{1,0:T(8,128)(2,1)S(1)}, bf16[768,512]{1,0:T(8,128)(2,1)S(1)}, u32[]{:S(2)}, u32[]{:S(2)}) collective-permute-start(bf16[768,512]{1,0:T(8,128)(2,1)S(1)} %get-tuple-element.94.refs_0_), channel_id=1, source_target_pairs={{0,8},{4,12},{8,0},{12,4},{16,24},{20,28},{24,16},{28,20},{1,9},{5... | collective-permute-start | bytes 2359304 | tf_op jit(solution)/shard_map/ppermute | solution.py:320
  140.1 38.7 %collective-permute-start.27 = (bf16[768,512]{1,0:T(8,128)(2,1)S(1)}, bf16[768,512]{1,0:T(8,128)(2,1)S(1)}, u32[]{:S(2)}, u32[]{:S(2)}) collective-permute-start(bf16[768,512]{1,0:T(8,128)(2,1)S(1)} %get-tuple-element.94.refs_0_), channel_id=1, source_target_pairs={{0,16},{4,20},{8,24},{12,28},{16,0},{20,4},{24,8},{28,12},{1,17},{... | collective-permute-start | bytes 2359304 | tf_op jit(solution)/shard_map/ppermute | solution.py:320
  144.5 34.9 %collective-permute-start.29 = (bf16[768,512]{1,0:T(8,128)(2,1)S(1)}, bf16[768,512]{1,0:T(8,128)(2,1)S(1)}, u32[]{:S(2)}, u32[]{:S(2)}) collective-permute-start(bf16[768,512]{1,0:T(8,128)(2,1)S(1)} %get-tuple-element.94.refs_0_), channel_id=1, source_target_pairs={{0,24},{4,28},{8,16},{12,20},{16,8},{20,12},{24,0},{28,4},{1,25},{... | collective-permute-start | bytes 2359304 | tf_op jit(solution)/shard_map/ppermute | solution.py:320
  153.8 46.7 %collective-permute-start.11 = (bf16[64,6144]{1,0:T(8,128)(2,1)S(1)}, bf16[64,6144]{1,0:T(8,128)(2,1)S(1)}, u32[]{:S(2)}, u32[]{:S(2)}) collective-permute-start(bf16[64,6144]{1,0:T(8,128)(2,1)S(1)} %collective-permute-done.7.refs_4_.refs_0_), channel_id=1, source_target_pairs={{2,3},{6,7},{10,11},{14,15},{18,19},{22,23},{26,27},{30,31}} | collective-permute-start | bytes 2359304 | tf_op jit(solution)/shard_map/ppermute | solution.py:343
  200.4 33.4 %collective-permute-start.26 = (bf16[768,512]{1,0:T(8,128)(2,1)S(1)}, bf16[768,512]{1,0:T(8,128)(2,1)S(1)}, u32[]{:S(2)}, u32[]{:S(2)}) collective-permute-start(bf16[768,512]{1,0:T(8,128)(2,1)S(1)} %collective-permute-done.25.refs_2_), channel_id=1, source_target_pairs={{0,4},{4,0},{8,12},{12,8},{16,20},{20,16},{24,28},{28,24},{1,5},{5... | collective-permute-start | bytes 2359304 | tf_op jit(solution)/shard_map/ppermute | solution.py:320
  200.5 33.3 %collective-permute-start.28 = (bf16[768,512]{1,0:T(8,128)(2,1)S(1)}, bf16[768,512]{1,0:T(8,128)(2,1)S(1)}, u32[]{:S(2)}, u32[]{:S(2)}) collective-permute-start(bf16[768,512]{1,0:T(8,128)(2,1)S(1)} %collective-permute-done.27.refs_4_), channel_id=1, source_target_pairs={{0,4},{4,0},{8,12},{12,8},{16,20},{20,16},{24,28},{28,24},{1,5},{5... | collective-permute-start | bytes 2359304 | tf_op jit(solution)/shard_map/ppermute | solution.py:320
  200.9 33.7 %collective-permute-start.30 = (bf16[768,512]{1,0:T(8,128)(2,1)S(1)}, bf16[768,512]{1,0:T(8,128)(2,1)S(1)}, u32[]{:S(2)}, u32[]{:S(2)}) collective-permute-start(bf16[768,512]{1,0:T(8,128)(2,1)S(1)} %collective-permute-done.29.refs_6_), channel_id=1, source_target_pairs={{0,4},{4,0},{8,12},{12,8},{16,20},{20,16},{24,28},{28,24},{1,5},{5... | collective-permute-start | bytes 2359304 | tf_op jit(solution)/shard_map/ppermute | solution.py:320
  233.8 43.1 %collective-permute-start.33 = (bf16[128,768]{1,0:T(8,128)(2,1)}, bf16[128,768]{1,0:T(8,128)(2,1)S(1)}, u32[]{:S(2)}, u32[]{:S(2)}) collective-permute-start(bf16[128,768]{1,0:T(8,128)(2,1)} %get-tuple-element.98), channel_id=1, source_target_pairs={{0,12},{4,8},{8,4},{12,0},{16,28},{20,24},{24,20},{28,16},{1,13},{... | collective-permute-start | bytes 589832 | tf_op jit(solution)/shard_map/ppermute | solution.py:320
  233.8 43.1 %collective-permute-start.34 = (bf16[128,768]{1,0:T(8,128)(2,1)}, bf16[128,768]{1,0:T(8,128)(2,1)S(1)}, u32[]{:S(2)}, u32[]{:S(2)}) collective-permute-start(bf16[128,768]{1,0:T(8,128)(2,1)} %get-tuple-element.99), channel_id=1, source_target_pairs={{0,16},{4,20},{8,24},{12,28},{16,0},{20,4},{24,8},{28,12},{1,17},{... | collective-permute-start | bytes 589832 | tf_op jit(solution)/shard_map/ppermute | solution.py:320
  234.6 42.4 %collective-permute-start.35 = (bf16[128,768]{1,0:T(8,128)(2,1)}, bf16[128,768]{1,0:T(8,128)(2,1)S(1)}, u32[]{:S(2)}, u32[]{:S(2)}) collective-permute-start(bf16[128,768]{1,0:T(8,128)(2,1)} %get-tuple-element.100), channel_id=1, source_target_pairs={{0,20},{4,16},{8,28},{12,24},{16,4},{20,0},{24,12},{28,8},{1,21},{... | collective-permute-start | bytes 589832 | tf_op jit(solution)/shard_map/ppermute | solution.py:320
  235.8 41.1 %collective-permute-start.36 = (bf16[128,768]{1,0:T(8,128)(2,1)S(1)}, bf16[128,768]{1,0:T(8,128)(2,1)S(1)}, u32[]{:S(2)}, u32[]{:S(2)}) collective-permute-start(bf16[128,768]{1,0:T(8,128)(2,1)S(1)} %get-tuple-element.101), channel_id=1, source_target_pairs={{0,24},{4,28},{8,16},{12,20},{16,8},{20,12},{24,0},{28,4},{1,25},{... | collective-permute-start | bytes 589832 | tf_op jit(solution)/shard_map/ppermute | solution.py:320
  240.1 36.9 %collective-permute-start.37 = (bf16[128,768]{1,0:T(8,128)(2,1)S(1)}, bf16[128,768]{1,0:T(8,128)(2,1)S(1)}, u32[]{:S(2)}, u32[]{:S(2)}) collective-permute-start(bf16[128,768]{1,0:T(8,128)(2,1)S(1)} %get-tuple-element.102), channel_id=1, source_target_pairs={{0,28},{4,24},{8,20},{12,16},{16,12},{20,8},{24,4},{28,0},{1,29},{... | collective-permute-start | bytes 589832 | tf_op jit(solution)/shard_map/ppermute | solution.py:320
  298.6 43.2 %collective-permute-start.15 = (bf16[3,128,256]{2,1,0:T(8,128)(2,1)S(1)}, bf16[3,128,256]{2,1,0:T(8,128)(2,1)S(1)}, u32[]{:S(2)}, u32[]{:S(2)}) collective-permute-start(bf16[3,128,256]{2,1,0:T(8,128)(2,1)S(1)} %copy-done.68), channel_id=1, source_target_pairs={{0,3},{1,0},{2,1},{3,2},{4,7},{5,4},{6,5},{7,6},{8,11},{9,8},{10,9... | collective-permute-start | bytes 589832 | tf_op jit(solution)/shard_map/ppermute | solution.py:317
  300.7 43.2 %collective-permute-start.16 = (bf16[3,128,256]{2,1,0:T(8,128)(2,1)S(1)}, bf16[3,128,256]{2,1,0:T(8,128)(2,1)S(1)}, u32[]{:S(2)}, u32[]{:S(2)}) collective-permute-start(bf16[3,128,256]{2,1,0:T(8,128)(2,1)S(1)} %copy-done.66), channel_id=1, source_target_pairs={{0,2},{1,3},{2,0},{3,1},{4,6},{5,7},{6,4},{7,5},{8,10},{9,11},{10,... | collective-permute-start | bytes 589832 | tf_op jit(solution)/shard_map/ppermute | solution.py:317
  305.9 35.9 %collective-permute-start.23 = (bf16[3,128,256]{2,1,0:T(8,128)(2,1)}, bf16[3,128,256]{2,1,0:T(8,128)(2,1)S(1)}, u32[]{:S(2)}, u32[]{:S(2)}) collective-permute-start(bf16[3,128,256]{2,1,0:T(8,128)(2,1)} %copy-done.69), channel_id=1, source_target_pairs={{0,1},{1,2},{2,3},{3,0},{4,5},{5,6},{6,7},{7,4},{8,9},{9,10},{10,1... | collective-permute-start | bytes 589832 | tf_op jit(solution)/shard_map/ppermute | solution.py:317
  (119 other events, 1796.1 us)

commit v2 on v1

v2 whole, which is shorter than its diff:
```python
import functools
import math
import jax
import jax.numpy as jnp
from jax import lax
from jax.experimental import pallas as pl
from jax.experimental.pallas import tpu as pltpu
from jax.sharding import PartitionSpec as P

HEAD_DIM = 128
MAX_NORM = 768
EPS = 1e-06
CORES = 2
CHUNKS = 3
HALVES = 2
TOGETHER = 3
MIB = 1024 * 1024


ANY = pl.BlockSpec(memory_space=pl.ANY)
SMEM = pl.BlockSpec(memory_space=pltpu.SMEM)
VMEM = pl.BlockSpec(memory_space=pltpu.VMEM)


def run(body, outs, args, in_specs, out_specs, scratch=(), grid=None, room=0, alias=None):
    return pl.pallas_call(
        body,
        out_shape=outs,
        grid=() if grid is None else grid,
        in_specs=in_specs,
        out_specs=out_specs,
        scratch_shapes=list(scratch),
        input_output_aliases=alias or {},
        compiler_params=pltpu.CompilerParams(vmem_limit_bytes=min(room + 4 * MIB, 62 * MIB)),
    )(*args)


def size_of(*arrays):
    return sum(math.prod(x.shape) * x.dtype.itemsize for x in arrays)


def chunk_count(heads):
    return max(c for c in range(1, CHUNKS + 1) if heads % c == 0)


def dot(a, b, dims=(1, 0)):
    contract = (((dims[0],), (dims[1],)), ((), ()))
    return lax.dot_general(a, b, contract, preferred_element_type=jnp.float32)


def pack_body(place_ref, *refs, ways, width):
    rows, outs = refs[:3], refs[3:]
    place = place_ref[0]
    for step in range(ways):
        column = pl.multiple_of(lax.rem(place + step, ways) * width, 128)
        for which in range(3):
            outs[step][which] = rows[which][:, pl.ds(column, width)]


def unpack_body(place_ref, *refs, ways, width, start, size, finish):
    pieces, sems = refs[:ways], refs[-1]
    outs = refs[-8:-5] if finish else refs[-4:-1]
    copies = []
    for step, piece in enumerate(pieces):
        column = pl.multiple_of(lax.rem(place_ref[0] + step, ways) * width + start, 128)
        for which in range(3):
            target = outs[which].at[:, pl.ds(column, size)]
            copies.append(pltpu.make_async_copy(piece.at[which], target, sems.at[step, which]))
    for copy in copies:
        copy.start()
    if finish:
        grad_ref, q_ref, k_ref, norm_ref = refs[-5:-1]
        weight_ref, parts = refs[ways], refs[ways + 1 : ways + 1 + finish]
        total = sum(part[...] for part in parts)
        q_gain, k_gain = total[0:1], total[1:2]
        squares = total[2:3] + q_gain * q_gain + k_gain * k_gain
        norm = jnp.sqrt(jnp.sum(squares, axis=1, keepdims=True))
        factor = jnp.minimum(jnp.float32(1.0), MAX_NORM / (norm + EPS))
        grad_ref[...] = weight_ref[...] * factor
        q_ref[...] = q_gain * factor
        k_ref[...] = k_gain * factor
        norm_ref[...] = norm
    for copy in copies:
        copy.wait()


def item_of(place, index, ways):
    both = jnp.minimum(place, ways - 1 - place)
    paired = index <= 2 * both
    hops = jnp.where(paired, (index + 1) // 2, index - both)
    lefty = jnp.where(paired, index % 2 == 1, 2 * place > ways - 1)
    return hops, lefty


def slot_of(place, index, ways):
    if index == 0:
        return jnp.int32(0)
    hops, lefty = item_of(place, index, ways)
    return jnp.where(lefty, hops, ways - hops)


def d_attn_body(place_ref, *refs, index, ways, groups, hops_list, parts, rows, cols, aligned, span, emit):
    count = sum(parts) * (2 if index else 1)
    sources, weight = refs[:count], refs[count]
    outs, full = refs[count + 1 : -1], refs[-1]
    place, group = place_ref[0], place_ref[1]

    def take(pieces):
        height = rows // len(pieces)
        for i, piece in enumerate(pieces):
            full[i * height : (i + 1) * height, :] = piece[...]

    if index == 0:
        take(sources)
    else:
        hops, lefty = item_of(place, index, ways)
        at = 0
        for dist, number in zip(hops_list, parts):
            for side in range(2):
                here = jnp.logical_and(hops == dist, lefty == (side == 0))
                pl.when(here)(functools.partial(take, sources[at : at + number]))
                at += number

    part = weight[span[0] : span[1], :]
    outs[0][...] = dot(full[...], part, (1, 1)).astype(jnp.bfloat16)
    if not emit:
        return
    if aligned:
        for mask in range(groups):
            column = pl.multiple_of(lax.bitwise_xor(group, mask) * cols, 128)
            outs[1 + mask][...] = full[:, pl.ds(column, cols)]
    else:
        outs[1][...] = full[...]


def segments(place, lengths_ref, shape, dim, ways, rows):
    index = lax.broadcasted_iota(jnp.int32, shape, dim)
    source = place - lax.div(index, rows)
    source = jnp.where(source < 0, source + ways, source)
    position = source * rows + lax.rem(index, rows)
    seg = jnp.zeros(shape, jnp.int32)
    end = jnp.int32(0)
    for clip in range(lengths_ref.shape[1]):
        end = end + lengths_ref[0, clip]
        seg = seg + (position >= end).astype(jnp.int32)
    return seg


def norm_rows(raw, gain):
    wide = raw.astype(jnp.float32)
    inverse = lax.rsqrt(jnp.mean(wide * wide, axis=-1, keepdims=True) + EPS)
    unit = wide * inverse
    return unit, inverse, (unit * gain).astype(jnp.bfloat16)


def norm_back(unit, inverse, gain, d_norm):
    d_unit = d_norm * gain
    grad = inverse * (d_unit - unit * jnp.mean(unit * d_unit, axis=-1, keepdims=True))
    return grad.astype(jnp.bfloat16), jnp.sum(unit * d_norm, axis=0, keepdims=True)


def forward_body(place_ref, lengths_ref, *refs, ways, rows):
    pieces = refs[:ways]
    q_gain_ref, k_gain_ref, attn_t_ref, probs_ref = refs[ways:]
    total = ways * rows
    place = place_ref[0]
    scale = HEAD_DIM ** (-0.5)
    same = segments(place, lengths_ref, (total, 1), 0, ways, rows) == segments(
        place, lengths_ref, (1, total), 1, ways, rows
    )

    def gather(which):
        return jnp.concatenate([piece[which] for piece in pieces], axis=0)

    _, _, q_norm = norm_rows(gather(0), q_gain_ref[...])
    _, _, k_norm = norm_rows(gather(1), k_gain_ref[...])
    value = gather(2)
    scores = dot(k_norm, q_norm, (1, 1)) * scale
    expo = jnp.where(same, jnp.exp(scores), 0.0)
    inverse_sum = 1.0 / jnp.sum(expo, axis=0, keepdims=True)
    probs = (expo * inverse_sum).astype(jnp.bfloat16)
    probs_ref[0] = probs
    attn_t_ref[...] = dot(value.T, probs).astype(jnp.bfloat16)


def backward_body(place_ref, *refs, ways, rows, heads):
    pieces = refs[:ways]
    d_pieces = refs[ways : 2 * ways]
    probs_ref, q_gain_ref, k_gain_ref, gains_ref = refs[2 * ways : 2 * ways + 4]
    outs = refs[2 * ways + 4 : 3 * ways + 4]
    d_attn_ref = refs[-1]
    place = place_ref[0]
    scale = HEAD_DIM ** (-0.5)
    for index in range(ways):
        row = pl.multiple_of(slot_of(place, index, ways) * rows, rows)
        d_attn_ref[pl.ds(row, rows), :] = d_pieces[index][...]
    q_gain = q_gain_ref[...]
    k_gain = k_gain_ref[...]
    q_sum = jnp.zeros((1, HEAD_DIM), jnp.float32)
    k_sum = jnp.zeros((1, HEAD_DIM), jnp.float32)
    for head in range(heads):
        part = slice(head * HEAD_DIM, (head + 1) * HEAD_DIM)

        def gather(which):
            return jnp.concatenate([piece[which, :, part] for piece in pieces], axis=0)

        q_unit, q_inv, q_norm = norm_rows(gather(0), q_gain)
        k_unit, k_inv, k_norm = norm_rows(gather(1), k_gain)
        value = gather(2)
        d_attn = d_attn_ref[:, part]
        probs = probs_ref[head]
        d_probs = dot(value, d_attn, (1, 1))
        probs32 = probs.astype(jnp.float32)
        row_sum = jnp.sum(probs32 * d_probs, axis=0, keepdims=True)
        d_scores = (probs32 * (d_probs - row_sum) * scale).astype(jnp.bfloat16)
        d_value = dot(probs, d_attn).astype(jnp.bfloat16)
        d_k = dot(d_scores, q_norm)
        d_q = dot(k_norm.T, d_scores).T
        q_grad, q_part = norm_back(q_unit, q_inv, q_gain, d_q)
        k_grad, k_part = norm_back(k_unit, k_inv, k_gain, d_k)
        q_sum = q_sum + q_part
        k_sum = k_sum + k_part
        for step in range(ways):
            block = slice(step * rows, (step + 1) * rows)
            outs[step][0, :, part] = q_grad[block]
            outs[step][1, :, part] = k_grad[block]
            outs[step][2, :, part] = d_value[block]
    gains_ref[...] = jnp.concatenate(
        [q_sum, k_sum, jnp.zeros((6, HEAD_DIM), jnp.float32)], axis=0
    )


def weight_body(place_ref, *refs, items, ways, groups, rows, first, last):
    attn = refs[:groups]
    columns = refs[groups : (1 + len(items)) * groups]
    outs = refs[-2:] if last else refs[-1:]
    gain_refs = refs[(1 + len(items)) * groups + 1 : -2]
    left = []
    for index in items:
        slot = pl.multiple_of(slot_of(place_ref[0], index, ways) * rows, 128)
        left += [piece[:, pl.ds(slot, rows)] for piece in attn]
    right = [piece[...] for piece in columns]
    total = dot(jnp.concatenate(left, axis=1), jnp.concatenate(right, axis=0))
    if not first:
        total = total + refs[(1 + len(items)) * groups][...]
    outs[0][...] = total
    if last:
        squares = jnp.sum(jnp.sum(total * total, axis=0, keepdims=True), axis=1, keepdims=True)
        gains = sum(ref[...] for ref in gain_refs)
        row = lax.broadcasted_iota(jnp.int32, gains.shape, 0)
        outs[1][...] = gains + jnp.where(row == 2, squares / HEAD_DIM, 0.0)


def weight_items(ways):
    count = ways - 1
    starts = range(0, count, TOGETHER)
    return [list(range(i, min(i + TOGETHER, count))) for i in starts] + [[count]]


def make_local(groups, ways):
    def local(
        query_rows, key_rows, value_rows, out_grad, clip_lengths, out_weight, query_gain, key_gain
    ):
        place = lax.axis_index("seq")
        group = lax.axis_index("dp")
        places = jnp.stack([place, group]).astype(jnp.int32)
        rows, features = query_rows.shape[1:]
        width = features // ways
        heads = width // HEAD_DIM
        count = chunk_count(heads)
        size = width // count
        model = out_grad.shape[2]
        cols = model // groups
        aligned = cols % 128 == 0
        total = ways * rows
        bf16 = jnp.bfloat16
        f32 = jnp.float32
        lanes = -(-cols // 128) * 128

        def struct(*shape, dtype=bf16):
            return jax.ShapeDtypeStruct(shape, dtype)

        def shift(x, step):
            return lax.ppermute(x, "seq", [(i, (i + step) % ways) for i in range(ways)])

        def partner(x, mask):
            return lax.ppermute(x, "dp", [(i, i ^ mask) for i in range(groups)])

        packed = run(
            functools.partial(pack_body, ways=ways, width=width),
            [struct(3, rows, width)] * ways,
            (places, query_rows[0], key_rows[0], value_rows[0]),
            [SMEM, VMEM, VMEM, VMEM],
            [VMEM] * ways,
            room=6 * size_of(query_rows),
        )
        pieces = [packed[0]] + [shift(packed[step], step) for step in range(1, ways)]

        extra = [struct(rows, cols)] * groups if aligned else [struct(rows, model)]
        right, left = [[out_grad[0]]], [[out_grad[0]]]
        d_attn, columns = [], []
        for index in range(ways):
            if index > 0:
                up = [(i, i + 1) for i in range(index - 1, ways - 1)]
                down = [(i, i - 1) for i in range(1, ways - index + 1)]
                if index == 2:
                    part = rows // HALVES
                    sent = [
                        [side[1][0][half * part : (half + 1) * part] for half in range(HALVES)]
                        for side in (right, left)
                    ]
                else:
                    sent = [right[-1], left[-1]]
                right.append([])
                left.append([])
                for half in range(len(sent[0])):
                    right[-1].append(lax.ppermute(sent[0][half], "seq", up))
                    left[-1].append(lax.ppermute(sent[1][half], "seq", down))
            hops_list = list(range((index + 1) // 2, index + 1)) if index else [0]
            sources = [x for dist in hops_list for side in (right, left) for x in side[dist]]
            if index == 0:
                sources = [out_grad[0]]

            def piece(span, emit):
                return run(
                    functools.partial(
                        d_attn_body,
                        index=index,
                        ways=ways,
                        groups=groups,
                        hops_list=hops_list,
                        parts=[len(right[dist]) for dist in hops_list],
                        rows=rows,
                        cols=cols,
                        aligned=aligned,
                        span=span,
                        emit=emit,
                    ),
                    [struct(rows, span[1] - span[0])] + (extra if emit else []),
                    (places, *sources, out_weight),
                    [SMEM] + [VMEM] * (len(sources) + 1),
                    [VMEM] * (1 + (len(extra) if emit else 0)),
                    [pltpu.VMEM((rows, model), bf16)],
                    room=size_of(out_weight, out_grad, out_grad, *sources),
                )

            lead = []
            if index == ways - 1 and count > 1:
                lead = piece((0, size), False)
            results = piece((size if lead else 0, width), True)
            d_attn.append((*lead, results[0]))
            blocks = results[1:]
            if not aligned:
                blocks = [
                    lax.dynamic_slice_in_dim(results[1], (group ^ mask) * cols, cols, 1)
                    for mask in range(groups)
                ]
            got = {mask: partner(blocks[mask], mask) for mask in reversed(range(1, groups))}
            columns.append([blocks[0]] + [got[mask] for mask in range(1, groups)])

        attn_t, probs = run(
            functools.partial(forward_body, ways=ways, rows=rows),
            [struct(width, total), struct(heads, total, total)],
            (places, clip_lengths, *pieces, query_gain[None], key_gain[None]),
            [SMEM, SMEM]
            + [pl.BlockSpec((3, rows, HEAD_DIM), lambda h: (0, 0, h))] * ways
            + [pl.BlockSpec((1, HEAD_DIM), lambda h: (0, 0))] * 2,
            [
                pl.BlockSpec((HEAD_DIM, total), lambda h: (h, 0)),
                pl.BlockSpec((1, total, total), lambda h: (h, 0, 0)),
            ],
            grid=(heads,),
            room=24 * total * total + 4 * MIB,
        )
        attn = [attn_t]
        for mask in range(1, groups):
            if mask % CORES:
                attn.append(partner(attn[mask - 1], 1))
            else:
                attn.append(partner(attn_t, mask))

        gains = []
        back = []
        for index in range(count):
            results = run(
                functools.partial(
                    backward_body, ways=ways, rows=rows, heads=size // HEAD_DIM
                ),
                [struct(8, HEAD_DIM, dtype=f32)] + [struct(3, rows, size)] * ways,
                (places, *pieces, *[x[-1 if index else 0] for x in d_attn], probs, query_gain[None], key_gain[None]),
                [SMEM]
                + [pl.BlockSpec((3, rows, size), lambda i, at=index: (0, 0, at))] * ways
                + [
                    pl.BlockSpec((rows, size), lambda i, at=max(0, index + 1 - len(x)): (0, at))
                    for x in d_attn
                ]
                + [pl.BlockSpec((size // HEAD_DIM, total, total), lambda i, at=index: (at, 0, 0))]
                + [pl.BlockSpec((1, HEAD_DIM), lambda i: (0, 0))] * 2,
                [pl.BlockSpec((8, HEAD_DIM), lambda i: (0, 0))]
                + [pl.BlockSpec((3, rows, size), lambda i: (0, 0, 0))] * ways,
                [pltpu.VMEM((total, size), bf16)],
                grid=(1,),
                room=(20 + 4 * (size // HEAD_DIM)) * total * total + 4 * MIB,
            )
            gains.append(results[0])
            grads = results[1:]
            back.append(grads[0])
            for step in range(1, ways):
                back.append(shift(grads[step], -step))

        weight_raw = None
        for items in weight_items(ways):
            first, last = weight_raw is None, items[-1] == ways - 1
            results = run(
                functools.partial(
                    weight_body,
                    items=items,
                    ways=ways,
                    groups=groups,
                    rows=rows,
                    first=first,
                    last=last,
                ),
                [struct(width, cols, dtype=f32)]
                + ([struct(8, HEAD_DIM, dtype=f32)] if last else []),
                (places, *attn)
                + tuple(x for index in items for x in columns[index])
                + (() if first else (weight_raw,))
                + (tuple(gains) if last else ()),
                [SMEM]
                + [VMEM]
                * ((1 + len(items)) * groups + (0 if first else 1) + (len(gains) if last else 0)),
                [VMEM] * (2 if last else 1),
                room=groups * (total * width + len(items) * rows * (lanes + width)) * 2
                + 12 * width * lanes,
            )
            weight_raw = results[0]

        parts = [results[1]]
        for axis, number in (("dp", groups), ("seq", ways)):
            mask = 1
            while mask < number:
                radix = 4 if mask * 4 <= number and (axis == "seq" or mask > 1) else 2
                sent = sum(parts[1:], parts[0])
                parts = [sent]
                for step in range(1, radix):
                    if axis == "dp":
                        parts.append(partner(sent, mask * step))
                    else:
                        aside = 0
                        pairs = [
                            (d * ways + i, (d ^ aside) * ways + (i ^ (mask * step)))
                            for d in range(groups)
                            for i in range(ways)
                        ]
                        parts.append(lax.ppermute(sent, ("dp", "seq"), pairs))
                mask *= radix
        outs = ()
        for index in range(count):
            last = index == count - 1
            pieces = back[index * ways : (index + 1) * ways]
            extra_in = (weight_raw, *parts) if last else ()
            extra_out = [struct(width, cols, dtype=f32)] + [
                struct(*shape, dtype=f32) for shape in ((1, HEAD_DIM), (1, HEAD_DIM), (1, 1))
            ]
            outs = run(
                functools.partial(
                    unpack_body,
                    ways=ways,
                    width=width,
                    start=index * size,
                    size=size,
                    finish=len(parts) if last else 0,
                ),
                [struct(rows, features)] * 3 + (extra_out if last else []),
                (places, *pieces, *extra_in, *outs),
                [SMEM] + [VMEM] * (ways + len(extra_in)) + [ANY] * len(outs),
                [ANY] * 3 + [VMEM] * (4 if last else 0),
                [pltpu.SemaphoreType.DMA((ways, 3))],
                room=2 * size_of(*pieces) + (8 * width * lanes if last else 0),
                alias={1 + ways + len(extra_in) + i: i for i in range(len(outs))},
            )
        *grads, weight_grad, q_gain, k_gain, norm = outs
        return (
            *[grad[None] for grad in grads],
            weight_grad,
            q_gain[0],
            k_gain[0],
            norm[0, 0],
        )

    return local


def solution(mesh):
    rows = P("dp", "seq", None)
    groups, ways = mesh.shape["dp"], mesh.shape["seq"]
    body = make_local(groups, ways)

    return jax.shard_map(
        body,
        mesh=mesh,
        in_specs=(rows, rows, rows, rows, P("dp", None), P("seq", None), P(), P()),
        out_specs=(rows, rows, rows, P("seq", "dp"), P(), P(), P()),
        check_vma=False,
    )
```

time: 359 us -> 324 us (0.903)
  local copies, waits for them, and re-layouts: 34 us -> 6.46 us
  waiting for transfers between devices: 167 us -> 187 us
  Pallas kernels: 62.6 us -> 43.7 us
  other arithmetic: 5.24 us -> 0.08 us
  between operations: 5.35 us -> 1.23 us
    ppermute x14 -> x13, waiting for transfers between devices: 85.2 us -> 36.8 us  [the longest x5 25.2 us: local(): left[-1].append(lax.ppermute(sent[1][half], 'seq', down))]
    ppermute x12, waiting for transfers between devices: 41.8 us -> 77.7 us  [shift(): return lax.ppermute(x, 'seq', [(i, (i + step) % ways) for i in range(ways)])]
    ppermute x38 -> x39, waiting for transfers between devices: 39.5 us -> 72.8 us  [partner(): return lax.ppermute(x, 'dp', [(i, i ^ mask) for i in range(groups)])]
    unnamed x158 -> x18, local copies, waits for them, and re-layouts: 31.4 us -> 6.25 us
    pallas_call x12 -> x15, Pallas kernels: 62.6 us -> 43.7 us  [run(): pl.pallas_call(body, out_shape=outs, grid=() if grid is None else grid, i...]
    mul x2 -> x0, other arithmetic: 3.85 us -> none  [the longest x1 3.33 us: local(): weight_grad = weight_raw * factor]
    ppermute x38 -> x39, starting transfers between devices: 31.5 us -> 29.7 us  [partner(): return lax.ppermute(x, 'dp', [(i, i ^ mask) for i in range(groups)])]
    ppermute x14 -> x13, starting transfers between devices: 27.5 us -> 27.8 us  [the longest x5 11.5 us: local(): right[-1].append(lax.ppermute(sent[0][half], 'seq', up))]
  transfers between devices with their start and end apart: 64 -> 64, of which waited for: 27 -> 25; matrix products, arithmetic and copies ran while one was open for 1% -> 0% of each run, Pallas kernels for 16% -> 13%
where the time goes in v2:
time: 324 us; the launch traced here: 320 us
  waiting for transfers between devices  187 us (58%)
  starting transfers between devices  80.9 us (25%)
  Pallas kernels  43.7 us (13%)
  local copies, waits for them, and re-layouts  6.46 us (2%)
    ppermute x12, waiting for transfers between devices, shift(): return lax.ppermute(x, 'seq', [(i, (i + step) % ways) for i in range(ways)])  77.7 us
    ppermute x39, waiting for transfers between devices, partner(): return lax.ppermute(x, 'dp', [(i, i ^ mask) for i in range(groups)])  72.8 us
    pallas_call x15, Pallas kernels, run(): pl.pallas_call(body, out_shape=outs, grid=() if grid is None else grid, i...  43.7 us
    ppermute x39, starting transfers between devices, partner(): return lax.ppermute(x, 'dp', [(i, i ^ mask) for i in range(groups)])  29.7 us
    ppermute x5, waiting for transfers between devices, local(): left[-1].append(lax.ppermute(sent[1][half], 'seq', down))  25.2 us
    ppermute x12, starting transfers between devices, shift(): return lax.ppermute(x, 'seq', [(i, (i + step) % ways) for i in range(ways)])  23.3 us
    ppermute x5, starting transfers between devices, local(): right[-1].append(lax.ppermute(sent[0][half], 'seq', up))  11.5 us
    ppermute x5, starting transfers between devices, local(): left[-1].append(lax.ppermute(sent[1][half], 'seq', down))  11.1 us
  transfers between devices with their start and end apart: 64, of which 25 were waited for; matrix products, arithmetic and copies ran while one was open for 0% of the time, Pallas kernels for 13%

profile of v2, /device:TPU:12, one launch (start us, length us, event | category | flops | bytes accessed | tf_op | source)
XLA Modules:
  0.0 319.7 jit_solution(12219106483374194306)
XLA Ops:
  3.0 3.5 %collective-permute-start.3 = (bf16[128,6144]{1,0:T(8,128)(2,1)}, bf16[128,6144]{1,0:T(8,128)(2,1)S(1)}, u32[]{:S(2)}, u32[]{:S(2)}) collective-permute-start(bf16[128,6144]{1,0:T(8,128)(2,1)} %bitcast.15), channel_id=1, source_target_pairs={{0,1},{1,2},{2,3},{4,5},{5,6},{6,7},{8,9},{9,10},{10,11},{12,13},{... | collective-permute-start | bytes 4718600 | tf_op jit(solution)/shard_map/ppermute | solution.py:317
  6.6 3.7 %copy-done = bf16[768,6144]{1,0:T(8,128)(2,1)S(1)} copy-done((bf16[768,6144]{1,0:T(8,128)(2,1)S(1)}, bf16[768,6144]{1,0:T(8,128)(2,1)}, u32[]{:S(2)}) %copy-start) | copy-done | bytes 9437208
  11.7 3.8 %shard_map.136 = (bf16[128,768]{1,0:T(8,128)(2,1)S(1)}, bf16[128,768]{1,0:T(8,128)(2,1)S(1)}, bf16[128,768]{1,0:T(8,128)(2,1)S(1)}, bf16[128,768]{1,0:T(8,128)(2...) custom-call(s32[2]{0:T(128)S(1)} %pad_add_fusion.place_ref, ...), custom_call_target="tpu_custom_call" | custom-call | tf_op jit(solution)/shard_map/pallas_call | solution.py:26
  27.1 52.3 %collective-permute-done.refs_1_ = bf16[3,128,768]{2,1,0:T(8,128)(2,1)S(1)} collective-permute-done((bf16[3,128,768]{2,1,0:T(8,128)(2,1)S(1)}, bf16[3,128,768]{2,1,0:T(8,128)(2,1)S(1)}, u32[]{:S(2)}, u32[]{:S(2)}) %collective-permute-start) | collective-permute-done | bytes 589856 | tf_op jit(solution)/shard_map/ppermute | solution.py:284
  79.9 10.7 %collective-permute-done.1.refs_2_ = bf16[3,128,768]{2,1,0:T(8,128)(2,1)S(1)} collective-permute-done((bf16[3,128,768]{2,1,0:T(8,128)(2,1)S(1)}, bf16[3,128,768]{2,1,0:T(8,128)(2,1)S(1)}, u32[]{:S(2)}, u32[]{:S(2)}) %collective-permute-start.1) | collective-permute-done | bytes 589856 | tf_op jit(solution)/shard_map/ppermute | solution.py:284
  92.1 6.8 %shard_map.140 = (bf16[768,512]{1,0:T(8,128)(2,1)S(1)}, bf16[6,512,512]{2,1,0:T(8,128)(2,1)S(1)}) custom-call(s32[2]{0:T(128)S(1)} %pad_add_fusion.place_ref, s32[1,4]{1,0:T(1,128)S(1)} %copy-done.8, bf16[3,128,768]{2,1,0:T(8,128)(2,1)S(1)} %get-tuple-element.79.refs_0_, bf16[3,128,768]{2,1,0:T(8,128)(2,1)S(1)} %collective-permute-done.refs_1_, ...), custom_call_target="tpu_custom_call" | custom-call | tf_op jit(solution)/shard_map/pallas_call | solution.py:26
  104.7 3.9 %shard_map.137 = (bf16[128,768]{1,0:T(8,128)(2,1)S(1)}, bf16[128,768]{1,0:T(8,128)(2,1)S(1)}, bf16[128,768]{1,0:T(8,128)(2,1)S(1)}, bf16[128,768]{1,0:T(8,128)(2...) custom-call(s32[2]{0:T(128)S(1)} %pad_add_fusion.place_ref, ...), custom_call_target="tpu_custom_call" | custom-call | tf_op jit(solution)/shard_map/pallas_call | solution.py:26
  108.6 32.8 %collective-permute-done.36.refs_15_ = bf16[128,768]{1,0:T(8,128)(2,1)S(1)} collective-permute-done((bf16[128,768]{1,0:T(8,128)(2,1)S(1)}, bf16[128,768]{1,0:T(8,128)(2,1)S(1)}, u32[]{:S(2)}, u32[]{:S(2)}) %collective-permute-start.36) | collective-permute-done | bytes 196640 | tf_op jit(solution)/shard_map/ppermute | solution.py:287
  145.7 3.5 %collective-permute-done.38.refs_18_ = bf16[128,768]{1,0:T(8,128)(2,1)S(1)} collective-permute-done((bf16[128,768]{1,0:T(8,128)(2,1)S(1)}, bf16[128,768]{1,0:T(8,128)(2,1)S(1)}, u32[]{:S(2)}, u32[]{:S(2)}) %collective-permute-start.38) | collective-permute-done | bytes 196640 | tf_op jit(solution)/shard_map/ppermute | solution.py:287
  149.2 3.3 %collective-permute-done.39.refs_19_ = bf16[128,768]{1,0:T(8,128)(2,1)S(1)} collective-permute-done((bf16[128,768]{1,0:T(8,128)(2,1)S(1)}, bf16[128,768]{1,0:T(8,128)(2,1)S(1)}, u32[]{:S(2)}, u32[]{:S(2)}) %collective-permute-start.39) | collective-permute-done | bytes 196640 | tf_op jit(solution)/shard_map/ppermute | solution.py:287
  161.0 6.5 %collective-permute-done.43.refs_23_ = bf16[128,768]{1,0:T(8,128)(2,1)S(1)} collective-permute-done((bf16[128,768]{1,0:T(8,128)(2,1)S(1)}, bf16[128,768]{1,0:T(8,128)(2,1)S(1)}, u32[]{:S(2)}, u32[]{:S(2)}) %collective-permute-start.43) | collective-permute-done | bytes 196640 | tf_op jit(solution)/shard_map/ppermute | solution.py:287
  167.5 4.3 %collective-permute-start.6 = (bf16[64,6144]{1,0:T(8,128)(2,1)S(1)}, bf16[64,6144]{1,0:T(8,128)(2,1)S(1)}, u32[]{:S(2)}, u32[]{:S(2)}) collective-permute-start(bf16[64,6144]{1,0:T(8,128)(2,1)S(1)} %get-tuple-element.153), channel_id=1, source_target_pairs={{1,2},{2,3},{5,6},{6,7},{9,10},{10,11},{13,14},{14,15},{17,18},{18... | collective-permute-start | bytes 2359304 | tf_op jit(solution)/shard_map/ppermute | solution.py:317
  177.8 13.9 %collective-permute-done.7.refs_4_.refs_2_ = bf16[64,6144]{1,0:T(8,128)(2,1)S(1)} collective-permute-done((bf16[64,6144]{1,0:T(8,128)(2,1)S(1)}, bf16[64,6144]{1,0:T(8,128)(2,1)S(1)}, u32[]{:S(2)}, u32[]{:S(2)}) %collective-permute-start.7) | collective-permute-done | bytes 786464 | tf_op jit(solution)/shard_map/ppermute | solution.py:318
  195.3 10.4 %collective-permute-done.5.refs_2_.refs_0_ = bf16[64,6144]{1,0:T(8,128)(2,1)S(1)} collective-permute-done((bf16[64,6144]{1,0:T(8,128)(2,1)S(1)}, bf16[64,6144]{1,0:T(8,128)(2,1)S(1)}, u32[]{:S(2)}, u32[]{:S(2)}) %collective-permute-start.5) | collective-permute-done | bytes 786464 | tf_op jit(solution)/shard_map/ppermute | solution.py:317
  206.5 4.1 %shard_map.138 = (bf16[128,768]{1,0:T(8,128)(2,1)S(1)}, bf16[128,768]{1,0:T(8,128)(2,1)S(1)}, bf16[128,768]{1,0:T(8,128)(2,1)S(1)}, bf16[128,768]{1,0:T(8,128)(2...) custom-call(s32[2]{0:T(128)S(1)} %pad_add_fusion.place_ref, ...), custom_call_target="tpu_custom_call" | custom-call | tf_op jit(solution)/shard_map/pallas_call | solution.py:26
  213.6 9.6 %collective-permute-done.11.refs_6_ = bf16[64,6144]{1,0:T(8,128)(2,1)S(1)} collective-permute-done((bf16[64,6144]{1,0:T(8,128)(2,1)S(1)}, bf16[64,6144]{1,0:T(8,128)(2,1)S(1)}, u32[]{:S(2)}, u32[]{:S(2)}) %collective-permute-start.11) | collective-permute-done | bytes 786464 | tf_op jit(solution)/shard_map/ppermute | solution.py:318
  230.6 8.8 %collective-permute-done.47.refs_28_ = bf16[128,768]{1,0:T(8,128)(2,1)S(1)} collective-permute-done((bf16[128,768]{1,0:T(8,128)(2,1)S(1)}, bf16[128,768]{1,0:T(8,128)(2,1)S(1)}, u32[]{:S(2)}, u32[]{:S(2)}) %collective-permute-start.47) | collective-permute-done | bytes 196640 | tf_op jit(solution)/shard_map/ppermute | solution.py:287
  253.4 4.8 %collective-permute-done.26.refs_12_ = bf16[128,768]{1,0:T(8,128)(2,1)S(1)} collective-permute-done((bf16[128,768]{1,0:T(8,128)(2,1)S(1)}, bf16[128,768]{1,0:T(8,128)(2,1)S(1)}, u32[]{:S(2)}, u32[]{:S(2)}) %collective-permute-start.26) | collective-permute-done | bytes 196640 | tf_op jit(solution)/shard_map/ppermute | solution.py:287
  258.2 5.9 %collective-permute-start.62 = (bf16[3,128,256]{2,1,0:T(8,128)(2,1)S(1)}, bf16[3,128,256]{2,1,0:T(8,128)(2,1)S(1)}, u32[]{:S(2)}, u32[]{:S(2)}) collective-permute-start(bf16[3,128,256]{2,1,0:T(8,128)(2,1)S(1)} %get-tuple-element.136), channel_id=1, source_target_pairs={{0,2},{1,3},{2,0},{3,1},{4,6},{5,7},{6,4},{7,5},{8,10},{9,11},{10,... | collective-permute-start | bytes 589832 | tf_op jit(solution)/shard_map/ppermute | solution.py:284
  269.4 4.4 %shard_map.142.refs_16_ = f32[768,768]{1,0:T(8,128)S(1)} custom-call(s32[2]{0:T(128)S(1)} %pad_add_fusion.place_ref, bf16[768,512]{1,0:T(8,128)(2,1)S(1)} %get-tuple-element.92.refs_0_, bf16[768,512]{1,0:T(8,128)(2,1)S(1)} %collective-permute-done.16.refs_1_, bf16[768,512]{1,0:T(8,128)(2,1)S(1)} %collective-permute-done.17.refs_2_, ...), custom_call_target="tpu_custom_call" | custom-call | tf_op jit(solution)/shard_map/pallas_call | solution.py:26
  294.6 5.3 %collective-permute-start.57 = (f32[8,128]{1,0:T(8,128)S(1)}, f32[8,128]{1,0:T(8,128)S(1)}, u32[]{:S(2)}, u32[]{:S(2)}) collective-permute-start(f32[8,128]{1,0:T(8,128)S(1)} %add_add_fusion.refs_5_), channel_id=1, source_target_pairs={{0,3},{1,2},{2,1},{3,0},{4,7},{5,6},{6,5},{7,4},{8,11},{9,10},{10,... | collective-permute-start | bytes 12296 | tf_op jit(solution)/shard_map/ppermute | solution.py:456
  299.9 7.0 %collective-permute-done.60.refs_3_ = bf16[3,128,256]{2,1,0:T(8,128)(2,1)S(1)} collective-permute-done((bf16[3,128,256]{2,1,0:T(8,128)(2,1)S(1)}, bf16[3,128,256]{2,1,0:T(8,128)(2,1)S(1)}, u32[]{:S(2)}, u32[]{:S(2)}) %collective-permute-start.60) | collective-permute-done | bytes 196640 | tf_op jit(solution)/shard_map/ppermute | solution.py:284
  306.9 5.4 %collective-permute-done.13.refs_1_ = bf16[3,128,256]{2,1,0:T(8,128)(2,1)S(1)} collective-permute-done((bf16[3,128,256]{2,1,0:T(8,128)(2,1)S(1)}, bf16[3,128,256]{2,1,0:T(8,128)(2,1)S(1)}, u32[]{:S(2)}, u32[]{:S(2)}) %collective-permute-start.13) | collective-permute-done | bytes 196640 | tf_op jit(solution)/shard_map/ppermute | solution.py:284
  316.6 2.9 shard_map.149
  (142 shorter events, 100.9 us)
Async XLA Ops:
  0.6 103.3 %collective-permute-start.4 = (bf16[128,6144]{1,0:T(8,128)(2,1)}, bf16[128,6144]{1,0:T(8,128)(2,1)S(1)}, u32[]{:S(2)}, u32[]{:S(2)}) collective-permute-start(bf16[128,6144]{1,0:T(8,128)(2,1)} %bitcast.14), channel_id=1, source_target_pairs={{1,0},{2,1},{3,2},{5,4},{6,5},{7,6},{9,8},{10,9},{11,10},{13,12},{... | collective-permute-start | bytes 4718600 | tf_op jit(solution)/shard_map/ppermute | solution.py:318
  3.0 101.0 %collective-permute-start.3 = (bf16[128,6144]{1,0:T(8,128)(2,1)}, bf16[128,6144]{1,0:T(8,128)(2,1)S(1)}, u32[]{:S(2)}, u32[]{:S(2)}) collective-permute-start(bf16[128,6144]{1,0:T(8,128)(2,1)} %bitcast.15), channel_id=1, source_target_pairs={{0,1},{1,2},{2,3},{4,5},{5,6},{6,7},{8,9},{9,10},{10,11},{12,13},{... | collective-permute-start | bytes 4718600 | tf_op jit(solution)/shard_map/ppermute | solution.py:317
  19.3 60.1 %collective-permute-start = (bf16[3,128,768]{2,1,0:T(8,128)(2,1)S(1)}, bf16[3,128,768]{2,1,0:T(8,128)(2,1)S(1)}, u32[]{:S(2)}, u32[]{:S(2)}) collective-permute-start(bf16[3,128,768]{2,1,0:T(8,128)(2,1)S(1)} %get-tuple-element.80), channel_id=1, source_target_pairs={{0,1},{1,2},{2,3},{3,0},{4,5},{5,6},{6,7},{7,4},{8,9},{9,10},{10,1... | collective-permute-start | bytes 1769480 | tf_op jit(solution)/shard_map/ppermute | solution.py:284
  23.4 67.2 %collective-permute-start.1 = (bf16[3,128,768]{2,1,0:T(8,128)(2,1)S(1)}, bf16[3,128,768]{2,1,0:T(8,128)(2,1)S(1)}, u32[]{:S(2)}, u32[]{:S(2)}) collective-permute-start(bf16[3,128,768]{2,1,0:T(8,128)(2,1)S(1)} %get-tuple-element.81), channel_id=1, source_target_pairs={{0,2},{1,3},{2,0},{3,1},{4,6},{5,7},{6,4},{7,5},{8,10},{9,11},{10,... | collective-permute-start | bytes 1769480 | tf_op jit(solution)/shard_map/ppermute | solution.py:284
  26.6 64.1 %collective-permute-start.2 = (bf16[3,128,768]{2,1,0:T(8,128)(2,1)S(1)}, bf16[3,128,768]{2,1,0:T(8,128)(2,1)S(1)}, u32[]{:S(2)}, u32[]{:S(2)}) collective-permute-start(bf16[3,128,768]{2,1,0:T(8,128)(2,1)S(1)} %get-tuple-element.82), channel_id=1, source_target_pairs={{0,3},{1,0},{2,1},{3,2},{4,7},{5,4},{6,5},{7,6},{8,11},{9,8},{10,9... | collective-permute-start | bytes 1769480 | tf_op jit(solution)/shard_map/ppermute | solution.py:284
  98.9 42.5 %collective-permute-start.21 = (bf16[768,512]{1,0:T(8,128)(2,1)S(1)}, bf16[768,512]{1,0:T(8,128)(2,1)S(1)}, u32[]{:S(2)}, u32[]{:S(2)}) collective-permute-start(bf16[768,512]{1,0:T(8,128)(2,1)S(1)} %get-tuple-element.92.refs_0_), channel_id=1, source_target_pairs={{0,24},{4,28},{8,16},{12,20},{16,8},{20,12},{24,0},{28,4},{1,25},{... | collective-permute-start | bytes 2359304 | tf_op jit(solution)/shard_map/ppermute | solution.py:287
  101.1 40.8 %collective-permute-start.19 = (bf16[768,512]{1,0:T(8,128)(2,1)S(1)}, bf16[768,512]{1,0:T(8,128)(2,1)S(1)}, u32[]{:S(2)}, u32[]{:S(2)}) collective-permute-start(bf16[768,512]{1,0:T(8,128)(2,1)S(1)} %get-tuple-element.92.refs_0_), channel_id=1, source_target_pairs={{0,16},{4,20},{8,24},{12,28},{16,0},{20,4},{24,8},{28,12},{1,17},{... | collective-permute-start | bytes 2359304 | tf_op jit(solution)/shard_map/ppermute | solution.py:287
  102.5 40.8 %collective-permute-start.17 = (bf16[768,512]{1,0:T(8,128)(2,1)S(1)}, bf16[768,512]{1,0:T(8,128)(2,1)S(1)}, u32[]{:S(2)}, u32[]{:S(2)}) collective-permute-start(bf16[768,512]{1,0:T(8,128)(2,1)S(1)} %get-tuple-element.92.refs_0_), channel_id=1, source_target_pairs={{0,8},{4,12},{8,0},{12,4},{16,24},{20,28},{24,16},{28,20},{1,9},{5... | collective-permute-start | bytes 2359304 | tf_op jit(solution)/shard_map/ppermute | solution.py:287
  104.0 39.5 %collective-permute-start.16 = (bf16[768,512]{1,0:T(8,128)(2,1)S(1)}, bf16[768,512]{1,0:T(8,128)(2,1)S(1)}, u32[]{:S(2)}, u32[]{:S(2)}) collective-permute-start(bf16[768,512]{1,0:T(8,128)(2,1)S(1)} %get-tuple-element.92.refs_0_), channel_id=1, source_target_pairs={{0,4},{4,0},{8,12},{12,8},{16,20},{20,16},{24,28},{28,24},{1,5},{5... | collective-permute-start | bytes 2359304 | tf_op jit(solution)/shard_map/ppermute | solution.py:287
  104.0 37.4 %collective-permute-start.36 = (bf16[128,768]{1,0:T(8,128)(2,1)S(1)}, bf16[128,768]{1,0:T(8,128)(2,1)S(1)}, u32[]{:S(2)}, u32[]{:S(2)}) collective-permute-start(bf16[128,768]{1,0:T(8,128)(2,1)S(1)} %get-tuple-element.108), channel_id=1, source_target_pairs={{0,28},{4,24},{8,20},{12,16},{16,12},{20,8},{24,4},{28,0},{1,29},{... | collective-permute-start | bytes 589832 | tf_op jit(solution)/shard_map/ppermute | solution.py:287
  158.1 33.6 %collective-permute-start.7 = (bf16[64,6144]{1,0:T(8,128)(2,1)S(1)}, bf16[64,6144]{1,0:T(8,128)(2,1)S(1)}, u32[]{:S(2)}, u32[]{:S(2)}) collective-permute-start(bf16[64,6144]{1,0:T(8,128)(2,1)S(1)} %get-tuple-element.152), channel_id=1, source_target_pairs={{1,0},{2,1},{5,4},{6,5},{9,8},{10,9},{13,12},{14,13},{17,16},{18,1... | collective-permute-start | bytes 2359304 | tf_op jit(solution)/shard_map/ppermute | solution.py:318
  167.5 27.1 %collective-permute-start.6 = (bf16[64,6144]{1,0:T(8,128)(2,1)S(1)}, bf16[64,6144]{1,0:T(8,128)(2,1)S(1)}, u32[]{:S(2)}, u32[]{:S(2)}) collective-permute-start(bf16[64,6144]{1,0:T(8,128)(2,1)S(1)} %get-tuple-element.153), channel_id=1, source_target_pairs={{1,2},{2,3},{5,6},{6,7},{9,10},{10,11},{13,14},{14,15},{17,18},{18... | collective-permute-start | bytes 2359304 | tf_op jit(solution)/shard_map/ppermute | solution.py:317
  171.8 34.0 %collective-permute-start.5 = (bf16[64,6144]{1,0:T(8,128)(2,1)S(1)}, bf16[64,6144]{1,0:T(8,128)(2,1)S(1)}, u32[]{:S(2)}, u32[]{:S(2)}) collective-permute-start(bf16[64,6144]{1,0:T(8,128)(2,1)S(1)} %get-tuple-element.154), channel_id=1, source_target_pairs={{1,2},{2,3},{5,6},{6,7},{9,10},{10,11},{13,14},{14,15},{17,18},{18... | collective-permute-start | bytes 2359304 | tf_op jit(solution)/shard_map/ppermute | solution.py:317
  174.1 36.4 %collective-permute-start.18 = (bf16[768,512]{1,0:T(8,128)(2,1)S(1)}, bf16[768,512]{1,0:T(8,128)(2,1)S(1)}, u32[]{:S(2)}, u32[]{:S(2)}) collective-permute-start(bf16[768,512]{1,0:T(8,128)(2,1)S(1)} %collective-permute-done.17.refs_2_), channel_id=1, source_target_pairs={{0,4},{4,0},{8,12},{12,8},{16,20},{20,16},{24,28},{28,24},{1,5},{5... | collective-permute-start | bytes 2359304 | tf_op jit(solution)/shard_map/ppermute | solution.py:287
  175.8 36.8 %collective-permute-start.12 = (bf16[64,6144]{1,0:T(8,128)(2,1)S(1)}, bf16[64,6144]{1,0:T(8,128)(2,1)S(1)}, u32[]{:S(2)}, u32[]{:S(2)}) collective-permute-start(bf16[64,6144]{1,0:T(8,128)(2,1)S(1)} %collective-permute-done.8.refs_5_.refs_3_), channel_id=1, source_target_pairs={{1,0},{5,4},{9,8},{13,12},{17,16},{21,20},{25,24},{29,28}} | collective-permute-start | bytes 2359304 | tf_op jit(solution)/shard_map/ppermute | solution.py:318
  191.7 31.5 %collective-permute-start.11 = (bf16[64,6144]{1,0:T(8,128)(2,1)S(1)}, bf16[64,6144]{1,0:T(8,128)(2,1)S(1)}, u32[]{:S(2)}, u32[]{:S(2)}) collective-permute-start(bf16[64,6144]{1,0:T(8,128)(2,1)S(1)} %collective-permute-done.7.refs_4_.refs_2_), channel_id=1, source_target_pairs={{1,0},{5,4},{9,8},{13,12},{17,16},{21,20},{25,24},{29,28}} | collective-permute-start | bytes 2359304 | tf_op jit(solution)/shard_map/ppermute | solution.py:318
  194.6 29.3 %collective-permute-start.10 = (bf16[64,6144]{1,0:T(8,128)(2,1)S(1)}, bf16[64,6144]{1,0:T(8,128)(2,1)S(1)}, u32[]{:S(2)}, u32[]{:S(2)}) collective-permute-start(bf16[64,6144]{1,0:T(8,128)(2,1)S(1)} %collective-permute-done.6.refs_3_.refs_1_), channel_id=1, source_target_pairs={{2,3},{6,7},{10,11},{14,15},{18,19},{22,23},{26,27},{30,31}} | collective-permute-start | bytes 2359304 | tf_op jit(solution)/shard_map/ppermute | solution.py:317
  242.7 23.8 %collective-permute-start.27 = (bf16[128,768]{1,0:T(8,128)(2,1)S(1)}, bf16[128,768]{1,0:T(8,128)(2,1)S(1)}, u32[]{:S(2)}, u32[]{:S(2)}) collective-permute-start(bf16[128,768]{1,0:T(8,128)(2,1)S(1)} %get-tuple-element.98), channel_id=1, source_target_pairs={{0,20},{4,16},{8,28},{12,24},{16,4},{20,0},{24,12},{28,8},{1,21},{... | collective-permute-start | bytes 589832 | tf_op jit(solution)/shard_map/ppermute | solution.py:287
  243.3 26.2 %collective-permute-start.28 = (bf16[128,768]{1,0:T(8,128)(2,1)S(1)}, bf16[128,768]{1,0:T(8,128)(2,1)S(1)}, u32[]{:S(2)}, u32[]{:S(2)}) collective-permute-start(bf16[128,768]{1,0:T(8,128)(2,1)S(1)} %get-tuple-element.99), channel_id=1, source_target_pairs={{0,24},{4,28},{8,16},{12,20},{16,8},{20,12},{24,0},{28,4},{1,25},{... | collective-permute-start | bytes 589832 | tf_op jit(solution)/shard_map/ppermute | solution.py:287
  246.6 29.7 %collective-permute-start.29 = (bf16[128,768]{1,0:T(8,128)(2,1)S(1)}, bf16[128,768]{1,0:T(8,128)(2,1)S(1)}, u32[]{:S(2)}, u32[]{:S(2)}) collective-permute-start(bf16[128,768]{1,0:T(8,128)(2,1)S(1)} %get-tuple-element.100), channel_id=1, source_target_pairs={{0,28},{4,24},{8,20},{12,16},{16,12},{20,8},{24,4},{28,0},{1,29},{... | collective-permute-start | bytes 589832 | tf_op jit(solution)/shard_map/ppermute | solution.py:287
  250.9 29.4 %collective-permute-start.61 = (bf16[3,128,256]{2,1,0:T(8,128)(2,1)S(1)}, bf16[3,128,256]{2,1,0:T(8,128)(2,1)S(1)}, u32[]{:S(2)}, u32[]{:S(2)}) collective-permute-start(bf16[3,128,256]{2,1,0:T(8,128)(2,1)S(1)} %get-tuple-element.135), channel_id=1, source_target_pairs={{0,3},{1,0},{2,1},{3,2},{4,7},{5,4},{6,5},{7,6},{8,11},{9,8},{10,9... | collective-permute-start | bytes 589832 | tf_op jit(solution)/shard_map/ppermute | solution.py:284
  286.8 25.5 %collective-permute-start.13 = (bf16[3,128,256]{2,1,0:T(8,128)(2,1)S(1)}, bf16[3,128,256]{2,1,0:T(8,128)(2,1)S(1)}, u32[]{:S(2)}, u32[]{:S(2)}) collective-permute-start(bf16[3,128,256]{2,1,0:T(8,128)(2,1)S(1)} %get-tuple-element.89), channel_id=1, source_target_pairs={{0,3},{1,0},{2,1},{3,2},{4,7},{5,4},{6,5},{7,6},{8,11},{9,8},{10,9... | collective-permute-start | bytes 589832 | tf_op jit(solution)/shard_map/ppermute | solution.py:284
  288.0 27.3 %collective-permute-start.14 = (bf16[3,128,256]{2,1,0:T(8,128)(2,1)S(1)}, bf16[3,128,256]{2,1,0:T(8,128)(2,1)S(1)}, u32[]{:S(2)}, u32[]{:S(2)}) collective-permute-start(bf16[3,128,256]{2,1,0:T(8,128)(2,1)S(1)} %get-tuple-element.90), channel_id=1, source_target_pairs={{0,2},{1,3},{2,0},{3,1},{4,6},{5,7},{6,4},{7,5},{8,10},{9,11},{10,... | collective-permute-start | bytes 589832 | tf_op jit(solution)/shard_map/ppermute | solution.py:284
  290.4 25.0 %collective-permute-start.15 = (bf16[3,128,256]{2,1,0:T(8,128)(2,1)S(1)}, bf16[3,128,256]{2,1,0:T(8,128)(2,1)S(1)}, u32[]{:S(2)}, u32[]{:S(2)}) collective-permute-start(bf16[3,128,256]{2,1,0:T(8,128)(2,1)S(1)} %get-tuple-element.91), channel_id=1, source_target_pairs={{0,1},{1,2},{2,3},{3,0},{4,5},{5,6},{6,7},{7,4},{8,9},{9,10},{10,1... | collective-permute-start | bytes 589832 | tf_op jit(solution)/shard_map/ppermute | solution.py:284
  (49 other events, 854.7 us)

commit v3 on v2

--- a/solution.py
+++ b/solution.py
@@ -11,7 +11,7 @@
 MAX_NORM = 768
 EPS = 1e-06
 CORES = 2
-CHUNKS = 3
+CHUNKS = 2
 HALVES = 2
 TOGETHER = 3
 MIB = 1024 * 1024
@@ -57,17 +57,27 @@
             outs[step][which] = rows[which][:, pl.ds(column, width)]
 
 
-def unpack_body(place_ref, *refs, ways, width, start, size, finish):
+def unpack_body(place_ref, *refs, ways, width, start, size, finish, early_steps):
+    early = dict(zip(early_steps, refs))
+    refs = refs[len(early_steps) :]
     pieces, sems = refs[:ways], refs[-1]
+    place = place_ref[0]
     outs = refs[-8:-5] if finish else refs[-4:-1]
     copies = []
     for step, piece in enumerate(pieces):
         column = pl.multiple_of(lax.rem(place_ref[0] + step, ways) * width + start, 128)
         for which in range(3):
             target = outs[which].at[:, pl.ds(column, size)]
-            copies.append(pltpu.make_async_copy(piece.at[which], target, sems.at[step, which]))
-    for copy in copies:
-        copy.start()
+            copy = pltpu.make_async_copy(piece.at[which], target, sems.at[step, which])
+            copies.append(copy)
+            if step not in early:
+                copy.start()
+                continue
+            source = early[step].at[which, :, start : start + size]
+            other = pltpu.make_async_copy(source, target, sems.at[step, which])
+            late = jnp.logical_or(at_end(place, ways), at_end(lax.rem(place + step, ways), ways))
+            pl.when(late)(copy.start)
+            pl.when(jnp.logical_not(late))(other.start)
     if finish:
         grad_ref, q_ref, k_ref, norm_ref = refs[-5:-1]
         weight_ref, parts = refs[ways], refs[ways + 1 : ways + 1 + finish]
@@ -84,6 +94,10 @@
         copy.wait()
 
 
+def at_end(place, ways):
+    return jnp.logical_or(place == 0, place == ways - 1)
+
+
 def item_of(place, index, ways):
     both = jnp.minimum(place, ways - 1 - place)
     paired = index <= 2 * both
@@ -99,7 +113,7 @@
     return jnp.where(lefty, hops, ways - hops)
 
 
-def d_attn_body(place_ref, *refs, index, ways, groups, hops_list, parts, rows, cols, aligned, span, emit):
+def d_attn_body(place_ref, *refs, index, ways, groups, hops_list, parts, rows, cols, aligned, span, emit, when):
     count = sum(parts) * (2 if index else 1)
     sources, weight = refs[:count], refs[count]
     outs, full = refs[count + 1 : -1], refs[-1]
@@ -113,6 +127,8 @@
     if index == 0:
         take(sources)
     else:
+        if when == "early":
+            take(sources[: parts[0]])
         hops, lefty = item_of(place, index, ways)
         at = 0
         for dist, number in zip(hops_list, parts):
@@ -121,8 +137,15 @@
                 pl.when(here)(functools.partial(take, sources[at : at + number]))
                 at += number
 
-    part = weight[span[0] : span[1], :]
-    outs[0][...] = dot(full[...], part, (1, 1)).astype(jnp.bfloat16)
+
+    def multiply():
+        part = weight[span[0] : span[1], :]
+        outs[0][...] = dot(full[...], part, (1, 1)).astype(jnp.bfloat16)
+
+    if when == "late":
+        pl.when(at_end(place, ways))(multiply)
+    else:
+        multiply()
     if not emit:
         return
     if aligned:
@@ -183,7 +206,26 @@
     attn_t_ref[...] = dot(value.T, probs).astype(jnp.bfloat16)
 
 
-def backward_body(place_ref, *refs, ways, rows, heads):
+def backward_body(place_ref, *refs, late, index, ways, **sizes):
+    if not late:
+        backward_rows(place_ref, refs, ways, **sizes)
+        return
+    before, rest = refs[: ways + 1], refs[ways + 1 :]
+    end = at_end(place_ref[0], ways)
+
+    @pl.when(end)
+    def _():
+        backward_rows(place_ref, rest, ways, **sizes)
+
+    @pl.when(jnp.logical_not(end))
+    def _():
+        outs = rest[2 * ways + 3 : -1]
+        outs[0][...] = before[0][...] if index == 0 else jnp.zeros_like(outs[0])
+        for step in range(ways):
+            outs[1 + step][...] = before[1 + step][...]
+
+
+def backward_rows(place_ref, refs, ways, rows, heads):
     pieces = refs[:ways]
     d_pieces = refs[ways : 2 * ways]
     probs_ref, q_gain_ref, k_gain_ref, gains_ref = refs[2 * ways : 2 * ways + 4]
@@ -321,7 +363,7 @@
             if index == 0:
                 sources = [out_grad[0]]
 
-            def piece(span, emit):
+            def piece(span, emit, when="", hops_list=hops_list, sources=sources):
                 return run(
                     functools.partial(
                         d_attn_body,
@@ -335,6 +377,7 @@
                         aligned=aligned,
                         span=span,
                         emit=emit,
+                        when=when,
                     ),
                     [struct(rows, span[1] - span[0])] + (extra if emit else []),
                     (places, *sources, out_weight),
@@ -345,8 +388,12 @@
                 )
 
             lead = []
-            if index == ways - 1 and count > 1:
-                lead = piece((0, size), False)
+            if index == ways - 1:
+                near = hops_list[:-1]
+                have = [x for dist in near for side in (right, left) for x in side[dist]]
+                early_piece = piece((0, size), False, "early", near, have)[0]
+                if count > 1:
+                    lead = piece((0, size), False, "late")
             results = piece((size if lead else 0, width), True)
             d_attn.append((*lead, results[0]))
             blocks = results[1:]
@@ -379,34 +426,70 @@
             else:
                 attn.append(partner(attn_t, mask))
 
+        def backward(index, size, late, d_pieces, before):
+            row_spec = pl.BlockSpec((3, rows, size), lambda i: (0, 0, index))
+            gain_specs = [pl.BlockSpec((1, HEAD_DIM), lambda i: (0, 0))] * 2
+            sum_spec = pl.BlockSpec((8, HEAD_DIM), lambda i: (0, 0))
+            return run(
+                functools.partial(
+                    backward_body,
+                    late=late,
+                    index=index,
+                    ways=ways,
+                    rows=rows,
+                    heads=size // HEAD_DIM,
+                ),
+                [struct(8, HEAD_DIM, dtype=f32)] + [struct(3, rows, size)] * ways,
+                (
+                    places,
+                    *before,
+                    *pieces,
+                    *[x for x, _ in d_pieces],
+                    probs,
+                    query_gain[None],
+                    key_gain[None],
+                ),
+                [SMEM]
+                + ([sum_spec] + [row_spec] * ways if late else [])
+                + [row_spec] * ways
+                + [pl.BlockSpec((rows, size), lambda i, b=b: (0, b)) for _, b in d_pieces]
+                + [pl.BlockSpec((size // HEAD_DIM, total, total), lambda i: (index, 0, 0))]
+                + gain_specs,
+                [sum_spec] + [pl.BlockSpec((3, rows, size), lambda i: (0, 0, 0))] * ways,
+                [pltpu.VMEM((total, size), bf16)],
+                grid=(1,),
+                room=(20 + 4 * (size // HEAD_DIM)) * total * total
+                + 8 * MIB
+                + 2 * size_of(*pieces) * size // width,
+            )
+
+        before = backward(
+            0, size, False, [(x[-1], 0) for x in d_attn[:-1]] + [(early_piece, 0)], ()
+        )
+        inner = range(1, ways - 1)
+        early, late_pairs = {}, {}
+        for step in range(1, ways):
+            pairs = [(i, (i - step) % ways) for i in range(ways)]
+            near = [pair for pair in pairs if pair[0] in inner and pair[1] in inner]
+            late_pairs[step] = [pair for pair in pairs if pair not in near]
+            if near:
+                early[step] = lax.ppermute(before[1 + step], "seq", near)
+
         gains = []
         back = []
         for index in range(count):
-            results = run(
-                functools.partial(
-                    backward_body, ways=ways, rows=rows, heads=size // HEAD_DIM
-                ),
-                [struct(8, HEAD_DIM, dtype=f32)] + [struct(3, rows, size)] * ways,
-                (places, *pieces, *[x[-1 if index else 0] for x in d_attn], probs, query_gain[None], key_gain[None]),
-                [SMEM]
-                + [pl.BlockSpec((3, rows, size), lambda i, at=index: (0, 0, at))] * ways
-                + [
-                    pl.BlockSpec((rows, size), lambda i, at=max(0, index + 1 - len(x)): (0, at))
-                    for x in d_attn
-                ]
-                + [pl.BlockSpec((size // HEAD_DIM, total, total), lambda i, at=index: (at, 0, 0))]
-                + [pl.BlockSpec((1, HEAD_DIM), lambda i: (0, 0))] * 2,
-                [pl.BlockSpec((8, HEAD_DIM), lambda i: (0, 0))]
-                + [pl.BlockSpec((3, rows, size), lambda i: (0, 0, 0))] * ways,
-                [pltpu.VMEM((total, size), bf16)],
-                grid=(1,),
-                room=(20 + 4 * (size // HEAD_DIM)) * total * total + 4 * MIB,
-            )
+            d_pieces = [
+                (x[-1 if index else 0], max(0, index + 1 - len(x))) for x in d_attn
+            ]
+            results = backward(index, size, index == 0, d_pieces, () if index else before)
             gains.append(results[0])
             grads = results[1:]
             back.append(grads[0])
             for step in range(1, ways):
-                back.append(shift(grads[step], -step))
+                if index == 0:
+                    back.append(lax.ppermute(grads[step], "seq", late_pairs[step]))
+                else:
+                    back.append(shift(grads[step], -step))
 
         weight_raw = None
         for items in weight_items(ways):
@@ -458,6 +541,7 @@
         outs = ()
         for index in range(count):
             last = index == count - 1
+            inner_rows = early if index == 0 else {}
             pieces = back[index * ways : (index + 1) * ways]
             extra_in = (weight_raw, *parts) if last else ()
             extra_out = [struct(width, cols, dtype=f32)] + [
@@ -471,14 +555,15 @@
                     start=index * size,
                     size=size,
                     finish=len(parts) if last else 0,
+                    early_steps=list(inner_rows),
                 ),
                 [struct(rows, features)] * 3 + (extra_out if last else []),
-                (places, *pieces, *extra_in, *outs),
-                [SMEM] + [VMEM] * (ways + len(extra_in)) + [ANY] * len(outs),
+                (places, *inner_rows.values(), *pieces, *extra_in, *outs),
+                [SMEM] + [VMEM] * (len(inner_rows) + ways + len(extra_in)) + [ANY] * len(outs),
                 [ANY] * 3 + [VMEM] * (4 if last else 0),
                 [pltpu.SemaphoreType.DMA((ways, 3))],
-                room=2 * size_of(*pieces) + (8 * width * lanes if last else 0),
-                alias={1 + ways + len(extra_in) + i: i for i in range(len(outs))},
+                room=2 * size_of(*pieces, *inner_rows.values()) + (8 * width * lanes if last else 0),
+                alias={1 + len(inner_rows) + ways + len(extra_in) + i: i for i in range(len(outs))},
             )
         *grads, weight_grad, q_gain, k_gain, norm = outs
         return (

time: 324 us -> 337 us (1.040)
  the two profiles are of different devices: /device:TPU:12 before, /device:TPU:0 now
where the time goes in v3:
time: 337 us; the launch traced here: 336 us
  waiting for transfers between devices  196 us (58%)
  starting transfers between devices  85.9 us (25%)
  Pallas kernels  46.6 us (14%)
  local copies, waits for them, and re-layouts  6.47 us (2%)
    ppermute x39, waiting for transfers between devices, partner(): return lax.ppermute(x, 'dp', [(i, i ^ mask) for i in range(groups)])  77 us
    ppermute x5, waiting for transfers between devices, local(): left[-1].append(lax.ppermute(sent[1][half], 'seq', down))  49.7 us
    ppermute x6, waiting for transfers between devices, shift(): return lax.ppermute(x, 'seq', [(i, (i + step) % ways) for i in range(ways)])  49.4 us
    pallas_call x15, Pallas kernels, run(): pl.pallas_call(body, out_shape=outs, grid=() if grid is None else grid, i...  46.6 us
    ppermute x39, starting transfers between devices, partner(): return lax.ppermute(x, 'dp', [(i, i ^ mask) for i in range(groups)])  34.9 us
    ppermute x6, starting transfers between devices, shift(): return lax.ppermute(x, 'seq', [(i, (i + step) % ways) for i in range(ways)])  20.3 us
    ppermute x3, waiting for transfers between devices, local(): parts.append(lax.ppermute(sent, ('dp', 'seq'), pairs))  19.8 us
    ppermute x3, starting transfers between devices, local(): back.append(lax.ppermute(grads[step], 'seq', late_pairs[step]))  10.7 us
  transfers between devices with their start and end apart: 63, of which 22 were waited for; matrix products, arithmetic and copies ran while one was open for 0% of the time, Pallas kernels for 13%

profile of v3, /device:TPU:0, one launch (start us, length us, event | category | flops | bytes accessed | tf_op | source)
XLA Modules:
  0.0 336.1 jit_solution(5745822092626681800)
XLA Ops:
  1.9 5.7 %collective-permute-start.3 = (bf16[128,6144]{1,0:T(8,128)(2,1)}, bf16[128,6144]{1,0:T(8,128)(2,1)S(1)}, u32[]{:S(2)}, u32[]{:S(2)}) collective-permute-start(bf16[128,6144]{1,0:T(8,128)(2,1)} %bitcast.15), channel_id=1, source_target_pairs={{0,1},{1,2},{2,3},{4,5},{5,6},{6,7},{8,9},{9,10},{10,11},{12,13},{... | collective-permute-start | bytes 4718600 | tf_op jit(solution)/shard_map/ppermute | solution.py:359
  7.7 3.7 %copy-done = bf16[768,6144]{1,0:T(8,128)(2,1)S(1)} copy-done((bf16[768,6144]{1,0:T(8,128)(2,1)S(1)}, bf16[768,6144]{1,0:T(8,128)(2,1)}, u32[]{:S(2)}) %copy-start) | copy-done | bytes 9437208
  12.8 3.8 %shard_map.136 = (bf16[128,768]{1,0:T(8,128)(2,1)S(1)}, bf16[128,768]{1,0:T(8,128)(2,1)S(1)}, bf16[128,768]{1,0:T(8,128)(2,1)S(1)}, bf16[128,768]{1,0:T(8,128)(2...) custom-call(s32[2]{0:T(128)S(1)} %pad_add_fusion.place_ref, ...), custom_call_target="tpu_custom_call" | custom-call | tf_op jit(solution)/shard_map/pallas_call | solution.py:26
  29.5 26.7 %collective-permute-done.refs_1_.refs_6_ = bf16[3,128,768]{2,1,0:T(8,128)(2,1)S(1)} collective-permute-done((bf16[3,128,768]{2,1,0:T(8,128)(2,1)S(1)}, bf16[3,128,768]{2,1,0:T(8,128)(2,1)S(1)}, u32[]{:S(2)}, u32[]{:S(2)}) %collective-permute-start) | collective-permute-done | bytes 589856 | tf_op jit(solution)/shard_map/ppermute | solution.py:326
  57.8 22.6 %collective-permute-done.1.refs_2_.refs_7_ = bf16[3,128,768]{2,1,0:T(8,128)(2,1)S(1)} collective-permute-done((bf16[3,128,768]{2,1,0:T(8,128)(2,1)S(1)}, bf16[3,128,768]{2,1,0:T(8,128)(2,1)S(1)}, u32[]{:S(2)}, u32[]{:S(2)}) %collective-permute-start.1) | collective-permute-done | bytes 589856 | tf_op jit(solution)/shard_map/ppermute | solution.py:326
  82.9 6.8 %shard_map.140 = (bf16[768,512]{1,0:T(8,128)(2,1)S(1)}, bf16[6,512,512]{2,1,0:T(8,128)(2,1)S(1)}) custom-call(s32[2]{0:T(128)S(1)} %pad_add_fusion.place_ref, s32[1,4]{1,0:T(1,128)S(1)} %copy-done.8, bf16[3,128,768]{2,1,0:T(8,128)(2,1)S(1)} %get-tuple-element.76.refs_0_.refs_5_, bf16[3,128,768]{2,1,0:T(8,128)(2,1)S(1)} %collective-permute-done.refs_1_.refs_6_, ...), custom_call_target="tpu_custom_call" | custom-call | tf_op jit(solution)/shard_map/pallas_call | solution.py:26
  95.4 3.9 %shard_map.137 = (bf16[128,768]{1,0:T(8,128)(2,1)S(1)}, bf16[128,768]{1,0:T(8,128)(2,1)S(1)}, bf16[128,768]{1,0:T(8,128)(2,1)S(1)}, bf16[128,768]{1,0:T(8,128)(2...) custom-call(s32[2]{0:T(128)S(1)} %pad_add_fusion.place_ref, ...), custom_call_target="tpu_custom_call" | custom-call | tf_op jit(solution)/shard_map/pallas_call | solution.py:26
  99.2 31.7 %collective-permute-done.36.refs_15_ = bf16[128,768]{1,0:T(8,128)(2,1)S(1)} collective-permute-done((bf16[128,768]{1,0:T(8,128)(2,1)S(1)}, bf16[128,768]{1,0:T(8,128)(2,1)S(1)}, u32[]{:S(2)}, u32[]{:S(2)}) %collective-permute-start.36) | collective-permute-done | bytes 196640 | tf_op jit(solution)/shard_map/ppermute | solution.py:329
  144.8 3.7 %collective-permute-done.41.refs_21_ = bf16[128,768]{1,0:T(8,128)(2,1)S(1)} collective-permute-done((bf16[128,768]{1,0:T(8,128)(2,1)S(1)}, bf16[128,768]{1,0:T(8,128)(2,1)S(1)}, u32[]{:S(2)}, u32[]{:S(2)}) %collective-permute-start.41) | collective-permute-done | bytes 196640 | tf_op jit(solution)/shard_map/ppermute | solution.py:329
  151.0 6.7 %collective-permute-done.43.refs_23_ = bf16[128,768]{1,0:T(8,128)(2,1)S(1)} collective-permute-done((bf16[128,768]{1,0:T(8,128)(2,1)S(1)}, bf16[128,768]{1,0:T(8,128)(2,1)S(1)}, u32[]{:S(2)}, u32[]{:S(2)}) %collective-permute-start.43) | collective-permute-done | bytes 196640 | tf_op jit(solution)/shard_map/ppermute | solution.py:329
  159.3 17.7 %collective-permute-done.8.refs_5_.refs_3_ = bf16[64,6144]{1,0:T(8,128)(2,1)S(1)} collective-permute-done((bf16[64,6144]{1,0:T(8,128)(2,1)S(1)}, bf16[64,6144]{1,0:T(8,128)(2,1)S(1)}, u32[]{:S(2)}, u32[]{:S(2)}) %collective-permute-start.8) | collective-permute-done | bytes 786464 | tf_op jit(solution)/shard_map/ppermute | solution.py:360
  178.3 15.6 %collective-permute-done.7.refs_4_.refs_2_ = bf16[64,6144]{1,0:T(8,128)(2,1)S(1)} collective-permute-done((bf16[64,6144]{1,0:T(8,128)(2,1)S(1)}, bf16[64,6144]{1,0:T(8,128)(2,1)S(1)}, u32[]{:S(2)}, u32[]{:S(2)}) %collective-permute-start.7) | collective-permute-done | bytes 786464 | tf_op jit(solution)/shard_map/ppermute | solution.py:360
  196.7 4.1 %shard_map.138 = (bf16[128,768]{1,0:T(8,128)(2,1)S(1)}, bf16[128,768]{1,0:T(8,128)(2,1)S(1)}, bf16[128,768]{1,0:T(8,128)(2,1)S(1)}, bf16[128,768]{1,0:T(8,128)(2...) custom-call(s32[2]{0:T(128)S(1)} %pad_add_fusion.place_ref, ...), custom_call_target="tpu_custom_call" | custom-call | tf_op jit(solution)/shard_map/pallas_call | solution.py:26
  202.8 6.4 %collective-permute-done.45.refs_26_ = bf16[128,768]{1,0:T(8,128)(2,1)S(1)} collective-permute-done((bf16[128,768]{1,0:T(8,128)(2,1)S(1)}, bf16[128,768]{1,0:T(8,128)(2,1)S(1)}, u32[]{:S(2)}, u32[]{:S(2)}) %collective-permute-start.45) | collective-permute-done | bytes 196640 | tf_op jit(solution)/shard_map/ppermute | solution.py:329
  212.1 14.8 %collective-permute-done.11.refs_6_ = bf16[64,6144]{1,0:T(8,128)(2,1)S(1)} collective-permute-done((bf16[64,6144]{1,0:T(8,128)(2,1)S(1)}, bf16[64,6144]{1,0:T(8,128)(2,1)S(1)}, u32[]{:S(2)}, u32[]{:S(2)}) %collective-permute-start.11) | collective-permute-done | bytes 786464 | tf_op jit(solution)/shard_map/ppermute | solution.py:360
  233.5 8.9 %collective-permute-done.48.refs_29_ = bf16[128,768]{1,0:T(8,128)(2,1)S(1)} collective-permute-done((bf16[128,768]{1,0:T(8,128)(2,1)S(1)}, bf16[128,768]{1,0:T(8,128)(2,1)S(1)}, u32[]{:S(2)}, u32[]{:S(2)}) %collective-permute-start.48) | collective-permute-done | bytes 196640 | tf_op jit(solution)/shard_map/ppermute | solution.py:329
  249.1 3.1 shard_map.144
  255.1 3.6 %collective-permute-done.26.refs_12_ = bf16[128,768]{1,0:T(8,128)(2,1)S(1)} collective-permute-done((bf16[128,768]{1,0:T(8,128)(2,1)S(1)}, bf16[128,768]{1,0:T(8,128)(2,1)S(1)}, u32[]{:S(2)}, u32[]{:S(2)}) %collective-permute-start.26) | collective-permute-done | bytes 196640 | tf_op jit(solution)/shard_map/ppermute | solution.py:329
  259.4 3.4 %shard_map.146 = (f32[8,128]{1,0:T(8,128)S(1)}, bf16[3,128,384]{2,1,0:T(8,128)(2,1)S(1)}, bf16[3,128,384]{2,1,0:T(8,128)(2,1)S(1)}, bf16[3,128,384]{2,1,0:T(8,128)(2,1)S(1)}, bf16[3,128,384]{2,1,0:T(8,128)(2,1)S(1)}) custom-call(s32[2]{0:T(128)S(1)} %pad_add_fusion.place_ref, f32[8,128]{1,0:T(8,128)S(1)} %get-tuple-element.122.refs_0_, ...), custom_call_target="tpu_custom_call" | custom-call | tf_op jit(solution)/shard_map/pallas_call | solution.py:26
  262.8 7.9 %collective-permute-start.60 = (bf16[3,128,384]{2,1,0:T(8,128)(2,1)S(1)}, bf16[3,128,384]{2,1,0:T(8,128)(2,1)S(1)}, u32[]{:S(2)}, u32[]{:S(2)}) collective-permute-start(bf16[3,128,384]{2,1,0:T(8,128)(2,1)S(1)} %get-tuple-element.132), channel_id=1, source_target_pairs={{0,3},{1,0},{3,2},{4,7},{5,4},{7,6},{8,11},{9,8},{11,10},{12,15},{... | collective-permute-start | bytes 884744 | tf_op jit(solution)/shard_map/ppermute | solution.py:490
  270.8 4.4 %shard_map.142.refs_16_ = f32[768,768]{1,0:T(8,128)S(1)} custom-call(s32[2]{0:T(128)S(1)} %pad_add_fusion.place_ref, bf16[768,512]{1,0:T(8,128)(2,1)S(1)} %get-tuple-element.89.refs_0_, bf16[768,512]{1,0:T(8,128)(2,1)S(1)} %collective-permute-done.16.refs_1_, bf16[768,512]{1,0:T(8,128)(2,1)S(1)} %collective-permute-done.17.refs_2_, ...), custom_call_target="tpu_custom_call" | custom-call | tf_op jit(solution)/shard_map/pallas_call | solution.py:26
  275.2 3.1 shard_map.141
  297.0 10.0 %collective-permute-start.14 = (bf16[3,128,384]{2,1,0:T(8,128)(2,1)S(1)}, bf16[3,128,384]{2,1,0:T(8,128)(2,1)S(1)}, u32[]{:S(2)}, u32[]{:S(2)}) collective-permute-start(bf16[3,128,384]{2,1,0:T(8,128)(2,1)S(1)} %get-tuple-element.87), channel_id=1, source_target_pairs={{0,2},{1,3},{2,0},{3,1},{4,6},{5,7},{6,4},{7,5},{8,10},{9,11},{10,... | collective-permute-start | bytes 884744 | tf_op jit(solution)/shard_map/ppermute | solution.py:326
  313.1 19.8 %collective-permute-done.56.refs_7_ = f32[8,128]{1,0:T(8,128)S(1)} collective-permute-done((f32[8,128]{1,0:T(8,128)S(1)}, f32[8,128]{1,0:T(8,128)S(1)}, u32[]{:S(2)}, u32[]{:S(2)}) %collective-permute-start.56) | collective-permute-done | bytes 4128 | tf_op jit(solution)/shard_map/ppermute | solution.py:539
  (140 shorter events, 96.5 us)
Async XLA Ops:
  0.6 93.3 %collective-permute-start.4 = (bf16[128,6144]{1,0:T(8,128)(2,1)}, bf16[128,6144]{1,0:T(8,128)(2,1)S(1)}, u32[]{:S(2)}, u32[]{:S(2)}) collective-permute-start(bf16[128,6144]{1,0:T(8,128)(2,1)} %bitcast.14), channel_id=1, source_target_pairs={{1,0},{2,1},{3,2},{5,4},{6,5},{7,6},{9,8},{10,9},{11,10},{13,12},{... | collective-permute-start | bytes 4718600 | tf_op jit(solution)/shard_map/ppermute | solution.py:360
  1.9 92.0 %collective-permute-start.3 = (bf16[128,6144]{1,0:T(8,128)(2,1)}, bf16[128,6144]{1,0:T(8,128)(2,1)S(1)}, u32[]{:S(2)}, u32[]{:S(2)}) collective-permute-start(bf16[128,6144]{1,0:T(8,128)(2,1)} %bitcast.15), channel_id=1, source_target_pairs={{0,1},{1,2},{2,3},{4,5},{5,6},{6,7},{8,9},{9,10},{10,11},{12,13},{... | collective-permute-start | bytes 4718600 | tf_op jit(solution)/shard_map/ppermute | solution.py:359
  20.6 35.6 %collective-permute-start = (bf16[3,128,768]{2,1,0:T(8,128)(2,1)S(1)}, bf16[3,128,768]{2,1,0:T(8,128)(2,1)S(1)}, u32[]{:S(2)}, u32[]{:S(2)}) collective-permute-start(bf16[3,128,768]{2,1,0:T(8,128)(2,1)S(1)} %get-tuple-element.77), channel_id=1, source_target_pairs={{0,1},{1,2},{2,3},{3,0},{4,5},{5,6},{6,7},{7,4},{8,9},{9,10},{10,1... | collective-permute-start | bytes 1769480 | tf_op jit(solution)/shard_map/ppermute | solution.py:326
  24.6 55.8 %collective-permute-start.1 = (bf16[3,128,768]{2,1,0:T(8,128)(2,1)S(1)}, bf16[3,128,768]{2,1,0:T(8,128)(2,1)S(1)}, u32[]{:S(2)}, u32[]{:S(2)}) collective-permute-start(bf16[3,128,768]{2,1,0:T(8,128)(2,1)S(1)} %get-tuple-element.78), channel_id=1, source_target_pairs={{0,2},{1,3},{2,0},{3,1},{4,6},{5,7},{6,4},{7,5},{8,10},{9,11},{10,... | collective-permute-start | bytes 1769480 | tf_op jit(solution)/shard_map/ppermute | solution.py:326
  28.1 52.3 %collective-permute-start.2 = (bf16[3,128,768]{2,1,0:T(8,128)(2,1)S(1)}, bf16[3,128,768]{2,1,0:T(8,128)(2,1)S(1)}, u32[]{:S(2)}, u32[]{:S(2)}) collective-permute-start(bf16[3,128,768]{2,1,0:T(8,128)(2,1)S(1)} %get-tuple-element.79), channel_id=1, source_target_pairs={{0,3},{1,0},{2,1},{3,2},{4,7},{5,4},{6,5},{7,6},{8,11},{9,8},{10,9... | collective-permute-start | bytes 1769480 | tf_op jit(solution)/shard_map/ppermute | solution.py:326
  56.2 33.4 %collective-permute-start.33 = (bf16[128,768]{1,0:T(8,128)(2,1)S(1)}, bf16[128,768]{1,0:T(8,128)(2,1)S(1)}, u32[]{:S(2)}, u32[]{:S(2)}) collective-permute-start(bf16[128,768]{1,0:T(8,128)(2,1)S(1)} %get-tuple-element.102), channel_id=1, source_target_pairs={{0,16},{4,20},{8,24},{12,28},{16,0},{20,4},{24,8},{28,12},{1,17},{... | collective-permute-start | bytes 589832 | tf_op jit(solution)/shard_map/ppermute | solution.py:329
  89.7 41.7 %collective-permute-start.21 = (bf16[768,512]{1,0:T(8,128)(2,1)S(1)}, bf16[768,512]{1,0:T(8,128)(2,1)S(1)}, u32[]{:S(2)}, u32[]{:S(2)}) collective-permute-start(bf16[768,512]{1,0:T(8,128)(2,1)S(1)} %get-tuple-element.89.refs_0_), channel_id=1, source_target_pairs={{0,24},{4,28},{8,16},{12,20},{16,8},{20,12},{24,0},{28,4},{1,25},{... | collective-permute-start | bytes 2359304 | tf_op jit(solution)/shard_map/ppermute | solution.py:329
  91.7 40.2 %collective-permute-start.19 = (bf16[768,512]{1,0:T(8,128)(2,1)S(1)}, bf16[768,512]{1,0:T(8,128)(2,1)S(1)}, u32[]{:S(2)}, u32[]{:S(2)}) collective-permute-start(bf16[768,512]{1,0:T(8,128)(2,1)S(1)} %get-tuple-element.89.refs_0_), channel_id=1, source_target_pairs={{0,16},{4,20},{8,24},{12,28},{16,0},{20,4},{24,8},{28,12},{1,17},{... | collective-permute-start | bytes 2359304 | tf_op jit(solution)/shard_map/ppermute | solution.py:329
  92.4 40.4 %collective-permute-start.17 = (bf16[768,512]{1,0:T(8,128)(2,1)S(1)}, bf16[768,512]{1,0:T(8,128)(2,1)S(1)}, u32[]{:S(2)}, u32[]{:S(2)}) collective-permute-start(bf16[768,512]{1,0:T(8,128)(2,1)S(1)} %get-tuple-element.89.refs_0_), channel_id=1, source_target_pairs={{0,8},{4,12},{8,0},{12,4},{16,24},{20,28},{24,16},{28,20},{1,9},{5... | collective-permute-start | bytes 2359304 | tf_op jit(solution)/shard_map/ppermute | solution.py:329
  93.9 40.7 %collective-permute-start.16 = (bf16[768,512]{1,0:T(8,128)(2,1)S(1)}, bf16[768,512]{1,0:T(8,128)(2,1)S(1)}, u32[]{:S(2)}, u32[]{:S(2)}) collective-permute-start(bf16[768,512]{1,0:T(8,128)(2,1)S(1)} %get-tuple-element.89.refs_0_), channel_id=1, source_target_pairs={{0,4},{4,0},{8,12},{12,8},{16,20},{20,16},{24,28},{28,24},{1,5},{5... | collective-permute-start | bytes 2359304 | tf_op jit(solution)/shard_map/ppermute | solution.py:329
  93.9 37.0 %collective-permute-start.36 = (bf16[128,768]{1,0:T(8,128)(2,1)S(1)}, bf16[128,768]{1,0:T(8,128)(2,1)S(1)}, u32[]{:S(2)}, u32[]{:S(2)}) collective-permute-start(bf16[128,768]{1,0:T(8,128)(2,1)S(1)} %get-tuple-element.105), channel_id=1, source_target_pairs={{0,28},{4,24},{8,20},{12,16},{16,12},{20,8},{24,4},{28,0},{1,29},{... | collective-permute-start | bytes 589832 | tf_op jit(solution)/shard_map/ppermute | solution.py:329
  143.5 33.5 %collective-permute-start.8 = (bf16[64,6144]{1,0:T(8,128)(2,1)S(1)}, bf16[64,6144]{1,0:T(8,128)(2,1)S(1)}, u32[]{:S(2)}, u32[]{:S(2)}) collective-permute-start(bf16[64,6144]{1,0:T(8,128)(2,1)S(1)} %get-tuple-element.145), channel_id=1, source_target_pairs={{1,0},{2,1},{5,4},{6,5},{9,8},{10,9},{13,12},{14,13},{17,16},{18,1... | collective-permute-start | bytes 2359304 | tf_op jit(solution)/shard_map/ppermute | solution.py:360
  148.5 45.4 %collective-permute-start.7 = (bf16[64,6144]{1,0:T(8,128)(2,1)S(1)}, bf16[64,6144]{1,0:T(8,128)(2,1)S(1)}, u32[]{:S(2)}, u32[]{:S(2)}) collective-permute-start(bf16[64,6144]{1,0:T(8,128)(2,1)S(1)} %get-tuple-element.146), channel_id=1, source_target_pairs={{1,0},{2,1},{5,4},{6,5},{9,8},{10,9},{13,12},{14,13},{17,16},{18,1... | collective-permute-start | bytes 2359304 | tf_op jit(solution)/shard_map/ppermute | solution.py:360
  157.7 37.5 %collective-permute-start.6 = (bf16[64,6144]{1,0:T(8,128)(2,1)S(1)}, bf16[64,6144]{1,0:T(8,128)(2,1)S(1)}, u32[]{:S(2)}, u32[]{:S(2)}) collective-permute-start(bf16[64,6144]{1,0:T(8,128)(2,1)S(1)} %get-tuple-element.147), channel_id=1, source_target_pairs={{1,2},{2,3},{5,6},{6,7},{9,10},{10,11},{13,14},{14,15},{17,18},{18... | collective-permute-start | bytes 2359304 | tf_op jit(solution)/shard_map/ppermute | solution.py:359
  158.4 37.5 %collective-permute-start.5 = (bf16[64,6144]{1,0:T(8,128)(2,1)S(1)}, bf16[64,6144]{1,0:T(8,128)(2,1)S(1)}, u32[]{:S(2)}, u32[]{:S(2)}) collective-permute-start(bf16[64,6144]{1,0:T(8,128)(2,1)S(1)} %get-tuple-element.148), channel_id=1, source_target_pairs={{1,2},{2,3},{5,6},{6,7},{9,10},{10,11},{13,14},{14,15},{17,18},{18... | collective-permute-start | bytes 2359304 | tf_op jit(solution)/shard_map/ppermute | solution.py:359
  159.1 41.6 %collective-permute-start.18 = (bf16[768,512]{1,0:T(8,128)(2,1)S(1)}, bf16[768,512]{1,0:T(8,128)(2,1)S(1)}, u32[]{:S(2)}, u32[]{:S(2)}) collective-permute-start(bf16[768,512]{1,0:T(8,128)(2,1)S(1)} %collective-permute-done.17.refs_2_), channel_id=1, source_target_pairs={{0,4},{4,0},{8,12},{12,8},{16,20},{20,16},{24,28},{28,24},{1,5},{5... | collective-permute-start | bytes 2359304 | tf_op jit(solution)/shard_map/ppermute | solution.py:329
  177.1 33.7 %collective-permute-start.12 = (bf16[64,6144]{1,0:T(8,128)(2,1)S(1)}, bf16[64,6144]{1,0:T(8,128)(2,1)S(1)}, u32[]{:S(2)}, u32[]{:S(2)}) collective-permute-start(bf16[64,6144]{1,0:T(8,128)(2,1)S(1)} %collective-permute-done.8.refs_5_.refs_3_), channel_id=1, source_target_pairs={{1,0},{5,4},{9,8},{13,12},{17,16},{21,20},{25,24},{29,28}} | collective-permute-start | bytes 2359304 | tf_op jit(solution)/shard_map/ppermute | solution.py:360
  193.9 33.0 %collective-permute-start.11 = (bf16[64,6144]{1,0:T(8,128)(2,1)S(1)}, bf16[64,6144]{1,0:T(8,128)(2,1)S(1)}, u32[]{:S(2)}, u32[]{:S(2)}) collective-permute-start(bf16[64,6144]{1,0:T(8,128)(2,1)S(1)} %collective-permute-done.7.refs_4_.refs_2_), channel_id=1, source_target_pairs={{1,0},{5,4},{9,8},{13,12},{17,16},{21,20},{25,24},{29,28}} | collective-permute-start | bytes 2359304 | tf_op jit(solution)/shard_map/ppermute | solution.py:360
  244.4 33.9 %collective-permute-start.28 = (bf16[128,768]{1,0:T(8,128)(2,1)S(1)}, bf16[128,768]{1,0:T(8,128)(2,1)S(1)}, u32[]{:S(2)}, u32[]{:S(2)}) collective-permute-start(bf16[128,768]{1,0:T(8,128)(2,1)S(1)} %get-tuple-element.96), channel_id=1, source_target_pairs={{0,24},{4,28},{8,16},{12,20},{16,8},{20,12},{24,0},{28,4},{1,25},{... | collective-permute-start | bytes 589832 | tf_op jit(solution)/shard_map/ppermute | solution.py:329
  252.3 39.0 %collective-permute-start.58 = (bf16[3,128,384]{2,1,0:T(8,128)(2,1)S(1)}, bf16[3,128,384]{2,1,0:T(8,128)(2,1)S(1)}, u32[]{:S(2)}, u32[]{:S(2)}) collective-permute-start(bf16[3,128,384]{2,1,0:T(8,128)(2,1)S(1)} %get-tuple-element.124.refs_2_), channel_id=1, source_target_pairs={{2,1},{6,5},{10,9},{14,13},{18,17},{22,21},{26,25},{30,29}} | collective-permute-start | bytes 884744 | tf_op jit(solution)/shard_map/ppermute | solution.py:476
  258.8 35.3 %collective-permute-start.59 = (bf16[3,128,384]{2,1,0:T(8,128)(2,1)S(1)}, bf16[3,128,384]{2,1,0:T(8,128)(2,1)S(1)}, u32[]{:S(2)}, u32[]{:S(2)}) collective-permute-start(bf16[3,128,384]{2,1,0:T(8,128)(2,1)S(1)} %get-tuple-element.126.refs_4_), channel_id=1, source_target_pairs={{1,2},{5,6},{9,10},{13,14},{17,18},{21,22},{25,26},{29,30}} | collective-permute-start | bytes 884744 | tf_op jit(solution)/shard_map/ppermute | solution.py:476
  262.8 44.2 %collective-permute-start.60 = (bf16[3,128,384]{2,1,0:T(8,128)(2,1)S(1)}, bf16[3,128,384]{2,1,0:T(8,128)(2,1)S(1)}, u32[]{:S(2)}, u32[]{:S(2)}) collective-permute-start(bf16[3,128,384]{2,1,0:T(8,128)(2,1)S(1)} %get-tuple-element.132), channel_id=1, source_target_pairs={{0,3},{1,0},{3,2},{4,7},{5,4},{7,6},{8,11},{9,8},{11,10},{12,15},{... | collective-permute-start | bytes 884744 | tf_op jit(solution)/shard_map/ppermute | solution.py:490
  294.1 38.8 %collective-permute-start.13 = (bf16[3,128,384]{2,1,0:T(8,128)(2,1)S(1)}, bf16[3,128,384]{2,1,0:T(8,128)(2,1)S(1)}, u32[]{:S(2)}, u32[]{:S(2)}) collective-permute-start(bf16[3,128,384]{2,1,0:T(8,128)(2,1)S(1)} %get-tuple-element.86), channel_id=1, source_target_pairs={{0,3},{1,0},{2,1},{3,2},{4,7},{5,4},{6,5},{7,6},{8,11},{9,8},{10,9... | collective-permute-start | bytes 884744 | tf_op jit(solution)/shard_map/ppermute | solution.py:326
  297.0 35.8 %collective-permute-start.14 = (bf16[3,128,384]{2,1,0:T(8,128)(2,1)S(1)}, bf16[3,128,384]{2,1,0:T(8,128)(2,1)S(1)}, u32[]{:S(2)}, u32[]{:S(2)}) collective-permute-start(bf16[3,128,384]{2,1,0:T(8,128)(2,1)S(1)} %get-tuple-element.87), channel_id=1, source_target_pairs={{0,2},{1,3},{2,0},{3,1},{4,6},{5,7},{6,4},{7,5},{8,10},{9,11},{10,... | collective-permute-start | bytes 884744 | tf_op jit(solution)/shard_map/ppermute | solution.py:326
  (48 other events, 848.8 us)
